TPU v7x, 256 devices: a whole 4x4x8 slice. The times are simulated.
256 devices in a mesh: gx: 32 (over z_lo, y, core), gy: 8 (over z_hi, x).
Axes of the slice: x: 4, y: 4, z: 8 (z_hi: 2, z_lo: 4; z = z_hi * 4 + z_lo), core: 2. Of those that a mesh axis runs over, the one named last changes fastest.
Arguments:
- e_field: float32 [3, 64, 256, 1024], P(None, None, 'gx', 'gy'), may hold values from -6 to 6
- h_field: float32 [3, 64, 256, 1024], P(None, None, 'gx', 'gy'), may hold values from -6 to 6
- material: int32 [64, 256, 1024], P(None, 'gx', 'gy'), may hold values from 0 to 7
- permittivity: float32 [8], replicated, may hold values from 1 to 12
- conductivity: float32 [8], replicated, may hold values from 0.05 to 2
- src_shift: int32 [2048, 2], P(('gx', 'gy')), may hold values from 0 to 128
- src_weight: float32 [2048], P(('gx', 'gy')), may hold values from 0.05 to 5
- pupil_mask: int32 [128, 128], replicated, may hold values 0 or 1
Outputs:
- image: float32 [512, 512], P(('gx', 'gy'))
- e_final: float32 [3, 64, 256, 1024], P(None, None, 'gx', 'gy')
- h_final: float32 [3, 64, 256, 1024], P(None, None, 'gx', 'gy')
All inputs are finite; a program needn't handle non-finite values.
Results may differ from a plain program's by a relative error of at most 0.0019.
Values may be sent and summed in bfloat16 or wider, within the bound.
No kernel may reach another device: no remote copies, remote signals or barrier semaphores. Data moves between devices by JAX's collectives and lax.ppermute only.
A program may use at most 128 MiB of HBM per device.

v0:
```python
import math

import jax
import jax.numpy as jnp
from jax import lax
from jax.sharding import Mesh
from jax.sharding import PartitionSpec as P

STEPS = 4
K = 256
PW = 128
IMG = 512
GX = ("gx_0", "gx_1", "gx_2")
GY = ("gy_0", "gy_1")
GX_GY = ("gx_0", "gx_1", "gx_2", "gy_0", "gy_1")


COURANT = 0.5


def extended(block, sides, width):
    for axis, dim in sides:
        count = lax.axis_size(axis)
        forward = [(i, i + 1) for i in range(count - 1)]
        backward = [(target, source) for source, target in forward]
        low = lax.ppermute(
            lax.slice_in_dim(block, block.shape[dim] - width, None, axis=dim), axis, forward
        )
        high = lax.ppermute(lax.slice_in_dim(block, 0, width, axis=dim), axis, backward)
        block = jnp.concatenate([low, block, high], axis=dim)
    return block


def in_blocks(x, dim, length):
    dims = x.shape
    parts = x.reshape(*dims[:dim], length, dims[dim] // length, *dims[dim + 1 :])
    return jnp.moveaxis(parts, dim, 0)


def edges_of(length, count):
    turn = length // count
    if turn >= 8:
        turn -= turn % 8
    return [turn * k for k in range(1, count)]


def sum_in_order(parts, axes, order):
    inside = parts.shape[1:]
    parts = parts.reshape(*(lax.axis_size(a) for a in axes), *inside)
    parts = jnp.moveaxis(parts, order, range(len(axes))).reshape(-1, *inside)
    for k in order:
        parts = lax.psum_scatter(parts, axes[k], scatter_dimension=0, tiled=True)
    return parts[0]


def spread_scatter(x, axes, dim):
    parts = in_blocks(x, dim, lax.axis_size(axes))
    split_at = max(range(1, max(2, parts.ndim - 1)), key=lambda d: parts.shape[d])
    count, done = (len(axes), [])
    for first, section in enumerate(
        jnp.split(parts, edges_of(parts.shape[split_at], count), axis=split_at)
    ):
        if section.size:
            order = [(first + k) % count for k in range(count)]
            done.append(sum_in_order(section, axes, order))
    return jnp.concatenate(done, axis=split_at - 1)


def coefficients(material, permittivity, conductivity):
    loss = conductivity / (2.0 * permittivity)
    keep_tab = (1.0 - loss) / (1.0 + loss)
    drive_tab = COURANT / (permittivity * (1.0 + loss))
    keep = jnp.zeros(material.shape, jnp.float32)
    drive = jnp.zeros(material.shape, jnp.float32)
    for index in range(permittivity.shape[0]):
        chosen = material == index
        keep = jnp.where(chosen, keep_tab[index], keep)
        drive = jnp.where(chosen, drive_tab[index], drive)
    return (keep, drive)


def zero_face(field, axis):
    shape = list(field.shape)
    shape[axis] = 1
    return jnp.zeros(shape, field.dtype)


def ahead(field, face, axis):
    count = field.shape[axis]
    return jnp.concatenate((lax.slice_in_dim(field, 1, count, axis=axis), face), axis=axis)


def behind(field, face, axis):
    count = field.shape[axis]
    return jnp.concatenate((face, lax.slice_in_dim(field, 0, count - 1, axis=axis)), axis=axis)


def magnetic(e, h, faces_x, faces_y):
    ex, ey, ez = (e[0], e[1], e[2])
    ey_x = ahead(ey, faces_x[0], 1)
    ez_x = ahead(ez, faces_x[1], 1)
    ex_y = ahead(ex, faces_y[0], 2)
    ez_y = ahead(ez, faces_y[1], 2)
    ex_z = ahead(ex, zero_face(ex, 0), 0)
    ey_z = ahead(ey, zero_face(ey, 0), 0)
    new_x = h[0] - COURANT * (ez_y - ez - (ey_z - ey))
    new_y = h[1] - COURANT * (ex_z - ex - (ez_x - ez))
    new_z = h[2] - COURANT * (ey_x - ey - (ex_y - ex))
    return jnp.stack((new_x, new_y, new_z))


def electric(e, h, keep, drive, faces_x, faces_y):
    hx, hy, hz = (h[0], h[1], h[2])
    hy_x = behind(hy, faces_x[0], 1)
    hz_x = behind(hz, faces_x[1], 1)
    hx_y = behind(hx, faces_y[0], 2)
    hz_y = behind(hz, faces_y[1], 2)
    hx_z = behind(hx, zero_face(hx, 0), 0)
    hy_z = behind(hy, zero_face(hy, 0), 0)
    new_x = keep * e[0] + drive * (hz - hz_y - (hy - hy_z))
    new_y = keep * e[1] + drive * (hx - hx_z - (hz - hz_x))
    new_z = keep * e[2] + drive * (hy - hy_x - (hx - hx_y))
    return jnp.stack((new_x, new_y, new_z))


def exit_spectrum(near, row_start, col_start, rows_all, cols_all, order):
    count_x = near.shape[1]
    count_y = near.shape[2]
    freqs = jnp.arange(order, dtype=jnp.int32) - order // 2
    cols = col_start + jnp.arange(count_y, dtype=jnp.int32)
    phase_y = jnp.mod(cols[:, None] * freqs[None, :], cols_all).astype(jnp.float32) * (
        2.0 * math.pi / cols_all
    )
    table_y = jnp.concatenate((jnp.cos(phase_y), -jnp.sin(phase_y)), axis=1)
    half = jnp.dot(near.reshape(2 * count_x, count_y), table_y, precision=lax.Precision.HIGHEST)
    half = half.reshape(2, count_x, 2 * order)
    rows = row_start + jnp.arange(count_x, dtype=jnp.int32)
    phase_x = jnp.mod(freqs[:, None] * rows[None, :], rows_all).astype(jnp.float32) * (
        2.0 * math.pi / rows_all
    )
    table_x = jnp.concatenate((jnp.cos(phase_x), jnp.sin(phase_x)), axis=0)
    blocks = jnp.einsum("ax,pxb->pab", table_x, half, precision=lax.Precision.HIGHEST)
    real = blocks[:, :order, :order] + blocks[:, order:, order:]
    imag = blocks[:, :order, order:] - blocks[:, order:, :order]
    stacked = jnp.stack((real[0], imag[0], real[1], imag[1]), axis=1)
    return stacked * (1.0 / math.sqrt(rows_all * cols_all))


def pupil_tables(window, pixels):
    offsets = jnp.arange(window, dtype=jnp.int32) - window // 2
    places = jnp.arange(pixels, dtype=jnp.int32)
    phase = jnp.mod(offsets[:, None] * places[None, :], pixels).astype(jnp.float32) * (
        2.0 * math.pi / pixels
    )
    cosine = jnp.cos(phase)
    sine = jnp.sin(phase)
    second = jnp.concatenate(
        (jnp.concatenate((cosine, sine), axis=1), jnp.concatenate((-sine, cosine), axis=1)), axis=0
    )
    row_cos = cosine.T / window
    row_sin = sine.T / window
    real_row = jnp.stack((row_cos, -row_sin), axis=2)
    imag_row = jnp.stack((row_sin, row_cos), axis=2)
    first = jnp.stack((real_row, imag_row)).reshape(2, pixels, 2 * window)
    return (second.astype(jnp.bfloat16), first.astype(jnp.bfloat16))


def pupil_halves(spectrum_b, shifts, pupil_mask, second, window, pixels):
    zero = jnp.zeros((), jnp.int32)

    def cut(shift):
        return lax.dynamic_slice(spectrum_b, (shift[0], zero, shift[1]), (window, 4, window))

    pieces = jax.vmap(cut)(shifts)
    pieces = pieces * pupil_mask.astype(jnp.bfloat16)[None, :, None, :]
    count = shifts.shape[0]
    arranged = (
        pieces.reshape(count, window, 2, 2, window)
        .transpose(0, 2, 1, 3, 4)
        .reshape(count * 2 * window, 2 * window)
    )
    halves = jnp.dot(arranged, second, preferred_element_type=jnp.float32).astype(jnp.bfloat16)
    return halves.reshape(count * 2, 2 * window, pixels)


def local(
    e_field, h_field, material, permittivity, conductivity, src_shift, src_weight, pupil_mask
):
    tile_x = e_field.shape[2]
    tile_y = e_field.shape[3]
    depth = e_field.shape[1]
    rows_all = tile_x * lax.axis_size(GX)
    cols_all = tile_y * lax.axis_size(GY)
    devices = lax.axis_size(GX) * lax.axis_size(GY)
    keep, drive = coefficients(material, permittivity, conductivity)
    stacked = jnp.concatenate((e_field, h_field, keep[None], drive[None]), axis=0)
    wide = extended(stacked, ((GX, 2), (GY, 3)), STEPS)
    e = wide[0:3]
    h = wide[3:6]
    keep_wide = wide[6]
    drive_wide = wide[7]
    rows_glob = (
        lax.axis_index(GX) * tile_x - STEPS + jnp.arange(tile_x + 2 * STEPS, dtype=jnp.int32)
    )
    cols_glob = (
        lax.axis_index(GY) * tile_y - STEPS + jnp.arange(tile_y + 2 * STEPS, dtype=jnp.int32)
    )
    inside_x = (rows_glob >= 0) & (rows_glob < rows_all)
    inside_y = (cols_glob >= 0) & (cols_glob < cols_all)
    inside = (inside_x[:, None] & inside_y[None, :]).astype(jnp.float32)
    for step in range(STEPS):
        faces_x = (zero_face(e[1], 1), zero_face(e[2], 1))
        faces_y = (zero_face(e[0], 2), zero_face(e[2], 2))
        h = magnetic(e, h, faces_x, faces_y) * inside
        faces_x = (zero_face(h[1], 1), zero_face(h[2], 1))
        faces_y = (zero_face(h[0], 2), zero_face(h[2], 2))
        e = electric(e, h, keep_wide, drive_wide, faces_x, faces_y)
    e_final = e[:, :, STEPS : STEPS + tile_x, STEPS : STEPS + tile_y]
    h_final = h[:, :, STEPS : STEPS + tile_x, STEPS : STEPS + tile_y]
    near = e_final[0:2, depth - 1]
    partial_value = exit_spectrum(
        near, lax.axis_index(GX) * tile_x, lax.axis_index(GY) * tile_y, rows_all, cols_all, K
    )
    spectrum_b = lax.psum(partial_value, GX_GY).astype(jnp.bfloat16)
    second, first = pupil_tables(PW, IMG)
    halves = pupil_halves(spectrum_b, src_shift, pupil_mask, second, PW, IMG)
    total_sources = src_shift.shape[0] * devices
    factors = jnp.repeat(src_weight / total_sources, 2)
    count = IMG // devices * lax.axis_size(GX_GY)
    rows = first.reshape(2 * count, 2 * PW)

    def add(total, item):
        field = jnp.dot(rows, item[0], preferred_element_type=jnp.float32)
        return (
            total + item[1] * (field[:count] * field[:count] + field[count:] * field[count:]),
            None,
        )

    total, _ = lax.scan(add, jnp.zeros((count, IMG), jnp.float32), (halves, factors))
    image = spread_scatter(total, GX_GY, 0)
    return (image, e_final, h_final)


def solution(mesh):
    finer = Mesh(mesh.devices.reshape(4, 4, 2, 2, 4), ("gx_0", "gx_1", "gx_2", "gy_0", "gy_1"))
    return jax.shard_map(
        local,
        mesh=finer,
        in_specs=(
            P(None, None, GX, GY),
            P(None, None, GX, GY),
            P(None, GX, GY),
            P(),
            P(),
            P(GX_GY, None),
            P(GX_GY),
            P(),
        ),
        out_specs=(P(GX_GY, None), P(None, None, GX, GY), P(None, None, GX, GY)),
        check_vma=False,
    )
```

profile of v0, /device:TPU:1, one launch (start us, length us, event | category | flops | bytes accessed | tf_op | source)
XLA Modules:
  0.0 483.8 jit_solution(17278177107995790645)
XLA Ops:
  9.9 6.4 %select_bitcast_fusion.1 = (f32[1,64,8,128]{3,2,1,0:T(8,128)S(1)}, pred[64,8,128]{2,1,0:T(8,128)(4,1)S(1)}, pred[64,8,128]{2,1,0:T(8,128)(4,1)S(1)}, pred[64,8,1...) fusion(f32[]{:T(128)} %bitcast.7, f32[]{:T(128)} %bitcast.6, ...), kind=kLoop, calls=%fused_computation.126 | loop fusion | flops 1048576 | bytes 1048608 | tf_op jit(solution)/shard_map/broadcast_in_dim | solution.py:196
  16.4 5.2 %select_bitcast_fusion = f32[1,64,8,128]{3,2,1,0:T(8,128)S(1)} fusion(pred[64,8,128]{2,1,0:T(8,128)(4,1)S(1)} %get-tuple-element.112, pred[64,8,128]{2,1,0:T(8,128)(4,1)S(1)} %get-tuple-element.111, pred[64,8,128]{2,1,0:T(8,128)(4,1)S(1)} %get-tuple-element.110, pred[64,8,128]{2,1,0:T(8,128)(4,1)S(1)} %get-tuple-element.109, ...), kind=kLoop, calls=%fused_computation.125 | loop fusion | flops 524288 | bytes 786464 | tf_op jit(solution)/shard_map/broadcast_in_dim | solution.py:196
  24.9 4.6 collective-permute-start
  42.2 2.5 fusion.41
  48.0 4.8 fusion.57
  52.8 3.8 copy.36
  56.6 4.0 collective-permute-start.2
  60.6 3.8 copy.37
  71.4 3.9 copy.38
  75.3 3.9 copy.39
  79.2 11.6 %pad_maximum_fusion = f32[8,64,16,136]{3,2,1,0:T(8,128)S(1)} fusion(f32[8,64,16,4]{3,2,1,0:T(8,128)} %copy.39, f32[8,64,4,128]{3,2,1,0:T(4,128)} %collective-permute-done.1, f32[1,64,8,128]{3,2,1,0:T(8,128)S(1)} %select_bitcast_fusion, f32[1,64,8,128]{3,2,1,0:T(8,128)S(1)} %get-tuple-element.104, f32[3,64,8,128]{3,2,1,0:T(8,128)S(1)} %copy-done.9, ...), kind=kLoop, calls=%fused_computation.12 | loop fusion | flops 7798784 | bytes 8912896 | tf_op jit(solution)/shard_map/concatenate | solution.py:30
  116.9 2.5 add_bitcast_fusion
  122.0 95.8 %all-reduce.63 = bf16[256,4,256]{0,2,1:T(8,128)(2,1)S(1)} all-reduce(f32[256,4,256]{0,2,1:T(8,128)S(1)} %maximum_multiply_fusion.4), channel_id=1, replica_groups=mesh['gx_0'=4,'gx_1'=4,'gx_2'=2,'gy_0'=2,'gy_1'=4] {'gx_0','gx_1','gx_2'..., use_global_device_ids=true, to_apply=%region_0.1 | all-reduce | flops 262144 | bytes 1572864 | tf_op jit(solution)/shard_map/psum | solution.py:224
  217.8 22.4 %while.12 = (s32[]{:T(128)}, bf16[256,4,256]{0,2,1:T(8,128)(2,1)S(1)}, s32[8,3]{0,1:T(4,128)S(1)}, bf16[8,128,4,128]{3,2,1,0:T(4,128)(2,1)}, s32[]{:T(128)}) while((s32[]{:T(128)}, bf16[256,4,256]{0,2,1:T(8,128)(2,1)S(1)}, s32[8,3]{0,1:T(4,128)S(1)}, bf16[8,128,4,128]{3,2,1,0:T(4,128)(2,1)}, s32[]{:T(128)}) %tuple.113), condition=%wide.while_cond, body=%wide.while_body.sunk | while | flops 2 | bytes 787057 | solution.py:172
  242.4 3.3 convolution_convert_fusion
  245.6 7.2 %reshape.234 = bf16[16,256,512]{2,1,0:T(8,128)(2,1)} reshape(bf16[2048,1024]{1,0:T(8,128)(2,1)} %convolution_convert_fusion) | data formatting | bytes 8388608 | tf_op jit(solution)/shard_map/reshape | solution.py:183
  252.8 55.5 %while.13 = (s32[]{:T(128)}, f32[512,512]{0,1:T(8,128)S(1)}, f32[16]{0:T(128)S(1)}, bf16[16,256,512]{2,1,0:T(8,128)(2,1)}, bf16[1024,256]{1,0:T(8,128)(2,1)}, /*index=5*/s32[]{:T(128)}, s32[]{:T(128)}) while((s32[]{:T(128)}, f32[512,512]{0,1:T(8,128)S(1)}, f32[16]{0:T(128)S(1)}, bf16[16,256,512]{2,1,0:T(8,128)(2,1)}, ...), condition=%wide.region_2.3_spmd.clone, body=%wide.region_1.2_spmd.clone.sunk | while | flops 270008320 | bytes 7078503 | solution.py:239
  310.4 3.0 copy.47
  314.7 45.7 %all-reduce.58.cloned.1.call-done = f32[256,2,512]{2,1,0:T(2,128)} async-done(((f32[256,2,512]{2,1,0:T(2,128)}), f32[256,2,512]{2,1,0:T(2,128)}) %all-reduce.58.cloned.1.call-update) | async-done | bytes 1048592
  366.5 47.4 %all-reduce.60.cloned.1.call-done = f32[64,2,512]{2,1,0:T(2,128)} async-done(((f32[64,2,512]{2,1,0:T(2,128)}), f32[64,2,512]{2,1,0:T(2,128)}) %all-reduce.60.cloned.1.call-update) | async-done | bytes 262160
  415.7 3.0 slice.583
  419.7 41.7 %all-reduce.62.cloned.1.call-done = f32[16,2,512]{2,1,0:T(2,128)} async-done(((f32[16,2,512]{2,1,0:T(2,128)}), f32[16,2,512]{2,1,0:T(2,128)}) %all-reduce.62.cloned.1.call-update) | async-done | bytes 65552
  462.2 5.9 %all-reduce.51 = f32[4,2,512]{2,1,0:T(2,128)S(1)} all-reduce(f32[4,2,512]{2,1,0:T(2,128)S(1)} %constant_dynamic-slice_fusion.3), channel_id=5, replica_groups=mesh['gx_0'=4,'gx_1'=4,'gx_2'=2,'gy_0'=2,'gy_1'=4] {'gx_2'}, use_global_device_ids=true, to_apply=%region_6.7.clone | all-reduce | flops 4096 | bytes 32768
  468.0 7.8 %all-reduce.52 = f32[2,2,512]{2,1,0:T(2,128)S(1)} all-reduce(f32[2,2,512]{2,1,0:T(2,128)S(1)} %constant_dynamic-slice_fusion.2), channel_id=6, replica_groups=mesh['gx_0'=4,'gx_1'=4,'gx_2'=2,'gy_0'=2,'gy_1'=4] {'gy_0'}, use_global_device_ids=true, to_apply=%region_7.8.clone | all-reduce | flops 2048 | bytes 16384
  (258 shorter events, 148.2 us)
Async XLA Ops:
  7.2 353.2 %all-reduce.58.cloned.1.call-start = ((), (), s32[]{:S(2)}) async-start(), calls=%async_computation | async-start | bytes 2097152
  23.1 8.4 %copy-start.21 = (s32[8,2]{0,1:T(2,128)S(1)}, s32[8,2]{0,1:T(2,128)}, u32[]{:S(2)}) copy-start(s32[8,2]{0,1:T(2,128)} %param.15) | copy-start | bytes 196
  23.1 10.1 %copy-start.22 = (f32[8]{0:T(128)S(1)}, f32[8]{0:T(128)}, u32[]{:S(2)}) copy-start(f32[8]{0:T(128)} %param.16) | copy-start | bytes 100
  23.1 22.8 %copy-start.9 = (f32[3,64,8,128]{3,2,1,0:T(8,128)S(1)}, f32[3,64,8,128]{3,2,1,0:T(8,128)}, u32[]{:S(2)}) copy-start(f32[3,64,8,128]{3,2,1,0:T(8,128)} %param.11) | copy-start | bytes 2359300
  23.1 22.8 %copy-start.10 = (f32[3,64,8,128]{3,2,1,0:T(8,128)S(1)}, f32[3,64,8,128]{3,2,1,0:T(8,128)}, u32[]{:S(2)}) copy-start(f32[3,64,8,128]{3,2,1,0:T(8,128)} %param.10) | copy-start | bytes 2359300
  24.9 19.8 %collective-permute-start = (f32[8,64,4,128]{3,2,1,0:T(4,128)}, f32[8,64,4,128]{3,2,1,0:T(4,128)S(1)}, u32[]{:S(2)}, u32[]{:S(2)}) collective-permute-start(f32[8,64,4,128]{3,2,1,0:T(4,128)} %get-tuple-element.166), channel_id=1, source_target_pairs={{0,8},{8,16},{16,24},{24,32},{32,40},{40,48},{48,56},{56,64},{64,7... | collective-permute-start | bytes 3145736 | tf_op jit(solution)/shard_map/ppermute | solution.py:26
  29.4 16.4 %collective-permute-start.1 = (f32[8,64,4,128]{3,2,1,0:T(4,128)}, f32[8,64,4,128]{3,2,1,0:T(4,128)}, u32[]{:S(2)}, u32[]{:S(2)}) collective-permute-start(f32[8,64,4,128]{3,2,1,0:T(4,128)} %get-tuple-element.167), channel_id=1, source_target_pairs={{8,0},{16,8},{24,16},{32,24},{40,32},{48,40},{56,48},{64,56},{72,6... | collective-permute-start | bytes 3145736 | tf_op jit(solution)/shard_map/ppermute | solution.py:29
  44.7 3.3 copy-start.11
  56.6 9.5 %copy-start.13 = (bf16[1,512,256]{1,2,0:T(8,128)(2,1)S(1)}, bf16[1,512,256]{1,2,0:T(8,128)(2,1)}, u32[]{:S(2)}) copy-start(bf16[1,512,256]{1,2,0:T(8,128)(2,1)} %stack.107) | copy-start | bytes 786436
  56.6 14.8 %collective-permute-start.2 = (f32[8,64,16,4]{1,2,3,0:T(8,128)}, f32[8,64,16,4]{1,2,3,0:T(8,128)}, u32[]{:S(2)}, u32[]{:S(2)}) collective-permute-start(f32[8,64,16,4]{1,2,3,0:T(8,128)} %copy.36), channel_id=1, source_target_pairs={{0,1},{1,2},{2,3},{3,4},{4,5},{5,6},{6,7},{8,9},{9,10},{10,11},{11... | collective-permute-start | bytes 393224 | tf_op jit(solution)/shard_map/ppermute | solution.py:26
  64.4 10.9 %collective-permute-start.3 = (f32[8,64,16,4]{1,2,3,0:T(8,128)}, f32[8,64,16,4]{1,2,3,0:T(8,128)}, u32[]{:S(2)}, u32[]{:S(2)}) collective-permute-start(f32[8,64,16,4]{1,2,3,0:T(8,128)} %copy.37), channel_id=1, source_target_pairs={{1,0},{2,1},{3,2},{4,3},{5,4},{6,5},{7,6},{9,8},{10,9},{11,10},{12... | collective-permute-start | bytes 393224 | tf_op jit(solution)/shard_map/ppermute | solution.py:29
  116.8 3.0 copy-start.19
  217.8 24.6 %copy-start.14 = (bf16[128,512]{1,0:T(8,128)(2,1)S(1)}, bf16[128,512]{1,0:T(8,128)(2,1)}, u32[]{:S(2)}) copy-start(bf16[128,512]{1,0:T(8,128)(2,1)} %get-tuple-element.184) | copy-start | bytes 393220
  217.8 24.6 %copy-start.15 = (bf16[128,512]{1,0:T(8,128)(2,1)S(1)}, bf16[128,512]{1,0:T(8,128)(2,1)}, u32[]{:S(2)}) copy-start(bf16[128,512]{1,0:T(8,128)(2,1)} %get-tuple-element.185) | copy-start | bytes 393220
  308.7 4.7 copy-start.27
  308.7 53.4 %copy-start.26 = (u32[256]{0:T(256)S(1)}, u32[256]{0:T(256)}, u32[]{:S(2)}) copy-start(u32[256]{0:T(256)} %constant.260) | copy-start | bytes 3076
  308.7 54.0 %copy-start.25 = (u32[256]{0:T(256)S(1)}, u32[256]{0:T(256)}, u32[]{:S(2)}) copy-start(u32[256]{0:T(256)} %constant.264) | copy-start | bytes 3076
  308.7 54.6 %copy-start.24 = (u32[256]{0:T(256)S(1)}, u32[256]{0:T(256)}, u32[]{:S(2)}) copy-start(u32[256]{0:T(256)} %constant.268) | copy-start | bytes 3076
  308.7 55.2 %copy-start.23 = (u32[256]{0:T(256)S(1)}, u32[256]{0:T(256)}, u32[]{:S(2)}) copy-start(u32[256]{0:T(256)} %constant.272) | copy-start | bytes 3076
  308.7 106.7 %copy-start.6 = (f32[1,64,16,136]{3,2,0,1:T(8,128)S(1)}, f32[1,64,16,136]{3,2,0,1:T(8,128)}, u32[]{:S(2)}) copy-start(f32[1,64,16,136]{3,2,0,1:T(8,128)} %copy-done.5) | copy-start | bytes 1671172
  308.7 106.7 %copy-start.8 = (f32[1,64,16,136]{3,2,0,1:T(8,128)S(1)}, f32[1,64,16,136]{3,2,0,1:T(8,128)}, u32[]{:S(2)}) copy-start(f32[1,64,16,136]{3,2,0,1:T(8,128)} %copy-done.7) | copy-start | bytes 1671172
  310.4 105.1 %copy-start.12 = (f32[1,64,16,136]{3,2,0,1:T(8,128)S(1)}, f32[1,64,16,136]{3,2,0,1:T(8,128)}, u32[]{:S(2)}) copy-start(f32[1,64,16,136]{3,2,0,1:T(8,128)} %get-tuple-element.117) | copy-start | bytes 1671172
  313.4 100.6 %all-reduce.60.cloned.1.call-start = ((), (), s32[]{:S(2)}) async-start(), calls=%async_computation.1 | async-start | bytes 524288
  362.1 99.4 %all-reduce.62.cloned.1.call-start = ((), (), s32[]{:S(2)}) async-start(), calls=%async_computation.2 | async-start | bytes 131072
  (13 other events, 27.2 us)
Sparse Core Ops, SparseCore 0:
  313.5 46.8 all-reduce.57
  363.6 50.3 all-reduce.59
  416.3 45.1 all-reduce.61
where the time goes:
time: 492 us; the launch traced here: 484 us
  waiting for transfers between devices  136 us (28%)
  blocking collectives  109 us (22%)
  local copies, waits for them, and re-layouts  97.1 us (20%)
  other arithmetic  79.5 us (16%)
  matrix products  31.4 us (6%)
  between operations  17.4 us (4%)
  starting transfers between devices  12.3 us (2%)
    unnamed x6, waiting for transfers between devices  135 us
    psum x1, blocking collectives, local(): spectrum_b = lax.psum(partial_value, GX_GY).astype(jnp.bfloat16)  95.8 us
    dot_general x16, matrix products, add(): field = jnp.dot(rows, item[0], preferred_element_type=jnp.float32)  25.8 us
    gather x40, local copies, waits for them, and re-layouts  22.3 us
    add x16, other arithmetic, add(): total + item[1] * (field[:count] * field[:count] + field[count:] * field[...  19.9 us
    concatenate x2, other arithmetic, extended(): block = jnp.concatenate([low, block, high], axis=dim)  13.7 us
    unnamed x2, blocking collectives  13.7 us
    slice x3, local copies, waits for them, and re-layouts, extended(): lax.slice_in_dim(block, block.shape[dim] - width, None, axis=dim)  10.4 us
  transfers between devices with their start and end apart: 7, of which 4 were waited for; matrix products, arithmetic and copies ran while one was open for 7% of the time, Pallas kernels for 0%

commit v1 on v0

v1 whole, which is shorter than its diff:
```python
import numpy as np
import jax
import jax.numpy as jnp
from jax import lax
from jax.experimental import pallas as pl
from jax.experimental.pallas import tpu as pltpu
from jax.sharding import Mesh
from jax.sharding import PartitionSpec as P

STEPS = 4
COURANT = 0.5
NZ = 64
K = 256
PW = 128
IMG = 512
GRID = IMG // 2
MATS = 8
SOURCES = 2048
TOP = 5
BLOCK = 8
GX = ("zl", "y", "c")
GY = ("zh", "x")
ALL = GX + GY
F32 = jnp.float32
BF16 = jnp.bfloat16


def split_bf16(table):
    high = table.astype(np.float32).astype(jnp.bfloat16)
    low = (table - high.astype(np.float64)).astype(np.float32).astype(jnp.bfloat16)
    return high, low


def tables(rows_all, cols_all):
    freqs = np.arange(K) - K // 2
    phase_y = 2.0 * np.pi * (np.outer(np.arange(cols_all // 2), freqs) % cols_all) / cols_all
    ty = np.concatenate((np.cos(phase_y), -np.sin(phase_y)), axis=1)
    phase_x = 2.0 * np.pi * (np.outer(freqs, np.arange(rows_all)) % rows_all) / rows_all
    tx = np.concatenate((np.cos(phase_x), np.sin(phase_x)), axis=0)
    offsets = np.arange(PW) - PW // 2
    places = 2 * np.arange(GRID)
    phase = 2.0 * np.pi * (np.outer(offsets, places) % IMG) / IMG
    cosine, sine = np.cos(phase), np.sin(phase)
    seconds = []
    for half in range(2):
        c = cosine[:, half * 128 : half * 128 + 128]
        s = sine[:, half * 128 : half * 128 + 128]
        seconds.append(np.concatenate((np.concatenate((c, s), 1), np.concatenate((-s, c), 1)), 0))
    second = np.stack(seconds).astype(np.float32).astype(jnp.bfloat16)
    rc, rs = cosine.T / PW, sine.T / PW
    first = np.concatenate((np.concatenate((rc, -rs), 1), np.concatenate((rs, rc), 1)), 0)
    first = first.astype(np.float32).astype(jnp.bfloat16)
    lag = np.arange(-IMG, IMG + 1)
    orders = np.arange(1, GRID // 2)
    kernel = 1.0 + 2.0 * np.cos(2.0 * np.pi * np.outer(lag, orders) / IMG).sum(1)
    kernel = (kernel + np.cos(2.0 * np.pi * (GRID // 2) * lag / IMG)) / GRID
    between = np.arange(IMG)[:, None] - 2 * np.arange(GRID)[None, :]
    upsample = kernel[between + IMG]
    upsample[::2] = np.eye(GRID)
    return split_bf16(ty) + split_bf16(tx) + (second, first, upsample.astype(np.float32))


def sub_iota(shape):
    return lax.broadcasted_iota(jnp.int32, shape, len(shape) - 2)


def lane_iota(shape):
    return lax.broadcasted_iota(jnp.int32, shape, len(shape) - 1)


def pair_rows(near, far):
    turned = pltpu.roll(far, 4, axis=far.ndim - 2)
    low = sub_iota(near.shape) < 4
    return jnp.where(low, turned, near), jnp.where(low, near, turned)


def unpair_rows(up, down):
    low = sub_iota(up.shape) < 4
    near = jnp.where(low, down, up)
    far = pltpu.roll(jnp.where(low, up, down), 4, axis=up.ndim - 2)
    return near, far


def component(e_ref, h_ref, mat_ref, comp):
    if comp < 3:
        return e_ref[comp]
    if comp < 6:
        return h_ref[comp - 3]
    return (mat_ref[...] + 1).astype(F32)


def strip_kernel(e_ref, h_ref, mat_ref, shift_ref, weight_ref, low_ref, high_ref):
    slot = (lane_iota((4, 8, 128)) + 4) // 8 % 16
    first = lane_iota((2, 8, 128)) % 8 < 4
    for comp in range(7):
        layers = component(e_ref, h_ref, mat_ref, comp).reshape(4, 16, 8, 128)
        strip = layers[:, 0]
        for s in range(1, 16):
            strip = jnp.where(slot == s, pltpu.roll(layers[:, s], 8 * s, axis=2), strip)
        turned = pltpu.roll(strip[2:], 4, axis=2)
        low_ref[pl.ds(2 * comp, 2)] = jnp.where(first, strip[:2], turned)
        high_ref[pl.ds(2 * comp, 2)] = jnp.where(first, turned, strip[:2])
    row = sub_iota((8, 128))
    lane = lane_iota((8, 128))
    info = jnp.zeros((8, 128), F32)
    for s in range(8):
        here = row == s
        info = jnp.where(here & (lane == 0), shift_ref[0, s].astype(F32), info)
        info = jnp.where(here & (lane == 1), shift_ref[1, s].astype(F32), info)
        info = jnp.where(here & (lane == 2), weight_ref[s], info)
    low_ref[14] = info
    high_ref[14] = info


def rows_kernel(e_ref, h_ref, mat_ref, after_ref, up_ref, down_ref):
    for comp in range(7):
        block = component(e_ref, h_ref, mat_ref, comp)
        up, down = pair_rows(block[:32], block[32:])
        up_ref[comp] = up
        down_ref[comp] = down


def corner_kernel(low_ref, high_ref, own_ref, strip_ref, up_ref, down_ref):
    first = lane_iota((2, 8, 128)) % 8 < 4
    for comp in range(7):
        low = low_ref[pl.ds(2 * comp, 2)]
        high = high_ref[pl.ds(2 * comp, 2)]
        near = jnp.where(first, high, low)
        far = pltpu.roll(jnp.where(first, low, high), 124, axis=2)
        strip_ref[pl.ds(4 * comp, 2)] = near
        strip_ref[pl.ds(4 * comp + 2, 2)] = far
        up, down = pair_rows(near, far)
        up_ref[pl.ds(2 * comp, 2)] = up
        down_ref[pl.ds(2 * comp, 2)] = down
    odd = lax.axis_index("x") % 2 == 1
    other = jnp.where(odd, low_ref[14], high_ref[14])
    info = jnp.where(lane_iota((8, 128)) < 8, own_ref[14], pltpu.roll(other, 8, axis=1))
    strip_ref[28] = info
    up_ref[14] = info
    down_ref[14] = info


def lookup(code, eps_ref, sig_ref):
    keep = jnp.zeros(code.shape, F32)
    drive = jnp.zeros(code.shape, F32)
    one = jnp.ones((8, 128), F32)
    for index in range(MATS):
        eps = one * eps_ref[index]
        loss = (one * sig_ref[index]) / (2.0 * eps)
        keep_one = ((1.0 - loss) / (1.0 + loss))[:1, :1]
        drive_one = (COURANT / (eps * (1.0 + loss)))[:1, :1]
        chosen = code == index + 1.0
        keep = jnp.where(chosen, keep_one, keep)
        drive = jnp.where(chosen, drive_one, drive)
    return keep, drive


def wide(own, near_row, strip, corner, slot):
    turn = (128 - 8 * slot) % 128
    if turn:
        strip = pltpu.roll(strip, turn, axis=1)
        corner = pltpu.roll(corner, turn, axis=1)
    return jnp.concatenate(
        (jnp.concatenate((own, strip), axis=1), jnp.concatenate((near_row, corner), axis=1)), axis=0
    )


def ahead(field, axis):
    return pltpu.roll(field, field.shape[axis] - 1, axis=axis)


def behind(field, axis):
    return pltpu.roll(field, 1, axis=axis)


def magnetic(e, e_next, h, inside):
    ex, ey, ez = e
    new_x = h[0] - COURANT * (ahead(ez, 1) - ez - (e_next[1] - ey))
    new_y = h[1] - COURANT * (e_next[0] - ex - (ahead(ez, 0) - ez))
    new_z = h[2] - COURANT * (ahead(ey, 0) - ey - (ahead(ex, 1) - ex))
    return new_x * inside, new_y * inside, new_z * inside


def electric(e, h, h_last, keep, drive):
    hx, hy, hz = h
    new_x = keep * e[0] + drive * (hz - behind(hz, 1) - (hy - h_last[1]))
    new_y = keep * e[1] + drive * (hx - h_last[0] - (hz - behind(hz, 0)))
    new_z = keep * e[2] + drive * (hy - behind(hy, 0) - (hx - behind(hx, 1)))
    return new_x, new_y, new_z


def near_kernel(
    e_ref, h_ref, mat_ref, up_ref, down_ref, strip_ref, cup_ref, cdown_ref, eps_ref, sig_ref,
    near_ref, info_ref,
):
    fields = []
    for comp in range(7):
        _, far = unpair_rows(up_ref[comp], down_ref[comp])
        _, corner = unpair_rows(cup_ref[2 * comp + 1], cdown_ref[2 * comp + 1])
        strip = strip_ref[4 * comp + 3]
        layers = []
        for z in range(8 - TOP, 8):
            if comp < 3:
                own = e_ref[comp, z]
            elif comp < 6:
                own = h_ref[comp - 3, z]
            else:
                own = (mat_ref[z] + 1).astype(F32)
            layers.append(wide(own, far[z], strip, corner, 8 + z))
        fields.append(layers)
    e = [tuple(fields[c][z] for c in range(3)) for z in range(TOP)]
    h = [tuple(fields[c + 3][z] for c in range(3)) for z in range(TOP)]
    zero = jnp.zeros((16, 256), F32)
    coefs = []
    for z in range(TOP):
        code = fields[6][z]
        coefs.append(lookup(code, eps_ref, sig_ref) + ((code > 0.5).astype(F32),))
    for step in range(STEPS):
        for z in range(step, TOP):
            keep, drive, inside = coefs[z]
            e_next = e[z + 1] if z + 1 < TOP else (zero, zero)
            h[z] = magnetic(e[z], e_next, h[z], inside)
            if z > step:
                e[z] = electric(e[z], h[z], h[z - 1], keep, drive)
    for pol in range(2):
        tile = e[TOP - 1][pol][:8, :128].astype(BF16)
        near_ref[:, pol] = jnp.broadcast_to(tile, (16, 8, 8, 128))
    up = lax.axis_index("c") == 1
    other = jnp.where(up, cup_ref[14], cdown_ref[14])
    info_ref[...] = jnp.where(
        lane_iota((8, 128)) < 16, strip_ref[28], pltpu.roll(other, 16, axis=1)
    )


def yee_kernel(
    e_ref, h_ref, mat_ref, up_ref, down_ref, strip_ref, cup_ref, cdown_ref, eps_ref, sig_ref,
    e_out, h_out, e_s, h_s, c_s,
):
    for comp in range(3):
        e_s[comp, NZ] = jnp.zeros((16, 256), F32)
        h_s[comp, 0] = jnp.zeros((16, 256), F32)
    for comp in range(7):
        near, far = unpair_rows(up_ref[comp], down_ref[comp])
        c_near, c_far = unpair_rows(
            cup_ref[pl.ds(2 * comp, 2)], cdown_ref[pl.ds(2 * comp, 2)]
        )
        for z in range(NZ):
            group, slot = divmod(z, 16)
            rows = near[z] if z < 32 else far[z - 32]
            corner = c_near[group] if group < 2 else c_far[group - 2]
            if comp < 3:
                own = e_ref[comp, z]
            elif comp < 6:
                own = h_ref[comp - 3, z]
            else:
                own = (mat_ref[z] + 1).astype(F32)
            value = wide(own, rows, strip_ref[4 * comp + group], corner, slot)
            if comp < 3:
                e_s[comp, z] = value
            elif comp < 6:
                h_s[comp - 3, z + 1] = value
            else:
                c_s[2, z] = value

    def coef(z, carry):
        code = c_s[2, z]
        keep, drive = lookup(code, eps_ref, sig_ref)
        c_s[0, z] = keep
        c_s[1, z] = drive
        c_s[2, z] = (code > 0.5).astype(F32)
        return carry

    lax.fori_loop(0, NZ, coef, 0)

    def step(k, carry):
        def block(i, carry):
            first = i * BLOCK
            for j in range(BLOCK):
                z = first + j
                e = tuple(e_s[c, z] for c in range(3))
                e_next = (e_s[0, z + 1], e_s[1, z + 1])
                h = tuple(h_s[c, z + 1] for c in range(3))
                h = magnetic(e, e_next, h, c_s[2, z])
                for c in range(3):
                    h_s[c, z + 1] = h[c]
            for j in range(BLOCK):
                z = first + j
                e = tuple(e_s[c, z] for c in range(3))
                h = tuple(h_s[c, z + 1] for c in range(3))
                e = electric(e, h, (h_s[0, z], h_s[1, z]), c_s[0, z], c_s[1, z])
                for c in range(3):
                    e_s[c, z] = e[c]
            return carry

        return lax.fori_loop(0, NZ // BLOCK, block, carry)

    lax.fori_loop(0, STEPS, step, 0)
    for comp in range(3):
        e_out[comp] = e_s[comp, pl.ds(0, NZ), pl.ds(0, 8), pl.ds(0, 128)]
        h_out[comp] = h_s[comp, pl.ds(1, NZ), pl.ds(0, 8), pl.ds(0, 128)]


def dot(a, b):
    return jnp.dot(a, b, preferred_element_type=F32)


def cut(ref, a, b):
    turn = (128 - b) % 128
    first = pltpu.roll(ref[0, pl.ds(a, PW), :], turn, axis=1)
    second = pltpu.roll(ref[1, pl.ds(a, PW), :], turn, axis=1)
    lane = lane_iota((PW, 128))
    return jnp.where(lane + b < 128, first, second)


def image_kernel(
    place_ref, info_ref, recv_ref, tyh_ref, tyl_ref, txh_ref, txl_ref, second_ref, first_ref,
    up_ref, mask_ref, out_ref, near_s, re_s, im_s, half_s, acc_s,
):
    for j in range(8):
        tile = recv_ref[:, j].astype(F32).reshape(K, 128)
        near_s[pl.ds(K * (j // 4), K), pl.ds(128 * (j % 4), 128)] = tile.astype(BF16)
    near = near_s[...]
    both = dot(near, tyh_ref[...]) + dot(near, tyl_ref[...])
    half = both[:K] + jnp.where(lane_iota((1, 2 * K)) % 2 == 0, both[K:], -both[K:])
    half_h = half.astype(BF16)
    half_l = (half - half_h.astype(F32)).astype(BF16)
    blocks = dot(txh_ref[...], half_h) + (dot(txh_ref[...], half_l) + dot(txl_ref[...], half_h))
    scale = 1.0 / 512.0
    real = (blocks[:K, :K] + blocks[K:, K:]) * scale
    imag = (blocks[:K, K:] - blocks[K:, :K]) * scale
    real = real.astype(BF16).astype(F32)
    imag = imag.astype(BF16).astype(F32)
    for t in range(2):
        re_s[t] = real[:, 128 * t : 128 * t + 128]
        im_s[t] = imag[:, 128 * t : 128 * t + 128]
    mask = mask_ref[...].astype(F32)
    side = lax.axis_index("x") % 2

    def cuts(i, carry):
        for t in range(8):
            a = place_ref[t, 8 * i]
            b = place_ref[t, 8 * i + 1]
            window = jnp.concatenate(
                (cut(re_s, a, b) * mask, cut(im_s, a, b) * mask), axis=1
            ).astype(BF16)
            half = dot(window, second_ref[side]).astype(BF16)
            half_s[i, pl.ds(0, 128), pl.ds(128 * t, 128)] = half[:, :128]
            half_s[i, pl.ds(128, 128), pl.ds(128 * t, 128)] = half[:, 128:]
        return carry

    lax.fori_loop(0, 4, cuts, 0)
    acc_s[...] = jnp.zeros(acc_s.shape, F32)

    def fields(i, carry):
        field = dot(first_ref[...], half_s[i])
        power = field[:GRID] * field[:GRID] + field[GRID:] * field[GRID:]
        total = acc_s[...]
        for t in range(8):
            weight = info_ref[t, 8 * i + 2] * (1.0 / SOURCES)
            total = total + power[:, 128 * t : 128 * t + 128] * weight
        acc_s[...] = total
        return carry

    lax.fori_loop(0, 4, fields, 0)
    out_ref[...] = jnp.dot(
        up_ref[...], acc_s[...], precision=lax.Precision.HIGHEST, preferred_element_type=F32
    )


def sum_kernel(recv_ref, up_ref, out_ref):
    total = jnp.sum(recv_ref[...].reshape(64, 8, 128), axis=0)
    total = total + pltpu.roll(total, 4, axis=0)
    line = jnp.concatenate((total, pltpu.roll(total, 6, axis=0)), axis=1)
    full = lax.dot_general(
        line, up_ref[...], (((1,), (1,)), ((), ())), precision=lax.Precision.HIGHEST,
        preferred_element_type=F32,
    )
    out_ref[...] = full[:2]


def shifted(value, axes, by):
    count = lax.axis_size(axes)
    return lax.ppermute(value, axes, [(i, i + by) for i in range(count) if 0 <= i + by < count])


def local(
    e_field, h_field, material, permittivity, conductivity, src_shift, src_weight, pupil_mask
):
    rows_all = e_field.shape[2] * lax.axis_size(GX)
    cols_all = e_field.shape[3] * lax.axis_size(GY)
    tyh, tyl, txh, txl, second, first, upsample = tables(rows_all, cols_all)
    smem = pl.BlockSpec(memory_space=pltpu.SMEM)
    vmem = pl.BlockSpec(memory_space=pltpu.VMEM)

    def shape(*dims, dtype=F32):
        return jax.ShapeDtypeStruct(dims, dtype)

    to_low, to_high = pl.pallas_call(
        strip_kernel,
        out_shape=(shape(15, 8, 128), shape(15, 8, 128)),
        in_specs=[vmem, vmem, vmem, smem, smem],
        out_specs=(vmem, vmem),
        name="strip",
    )(e_field, h_field, material, src_shift.T, src_weight)
    low = shifted(to_high, GY, 1)
    high = shifted(to_low, GY, -1)
    up, down = pl.pallas_call(
        rows_kernel,
        out_shape=(shape(7, 32, 8, 128), shape(7, 32, 8, 128)),
        in_specs=[vmem, vmem, vmem, pl.BlockSpec(memory_space=pl.ANY)],
        out_specs=(vmem, vmem),
        name="rows",
    )(e_field, h_field, material, to_low)
    up_in = shifted(up, GX, 1)
    down_in = shifted(down, GX, -1)
    strip, cup, cdown = pl.pallas_call(
        corner_kernel,
        out_shape=(shape(29, 8, 128), shape(15, 8, 128), shape(15, 8, 128)),
        in_specs=[vmem] * 3,
        out_specs=(vmem,) * 3,
        name="corner",
    )(low, high, to_low)
    cup_in = shifted(cup, GX, 1)
    cdown_in = shifted(cdown, GX, -1)

    field = pl.BlockSpec((3, 8, 8, 128), lambda i: (0, 7, 0, 0))
    rows = pl.BlockSpec((7, 8, 8, 128), lambda i: (0, 3, 0, 0))
    near, info = pl.pallas_call(
        near_kernel,
        grid=(1,),
        out_shape=(shape(16, 2, 8, 8, 128, dtype=BF16), shape(8, 128)),
        in_specs=[
            field, field, pl.BlockSpec((8, 8, 128), lambda i: (7, 0, 0)), rows, rows,
            pl.BlockSpec((29, 8, 128), lambda i: (0, 0, 0)),
            pl.BlockSpec((15, 8, 128), lambda i: (0, 0, 0)),
            pl.BlockSpec((15, 8, 128), lambda i: (0, 0, 0)), smem, smem,
        ],
        out_specs=(
            pl.BlockSpec((16, 2, 8, 8, 128), lambda i: (0, 0, 0, 0, 0)),
            pl.BlockSpec((8, 128), lambda i: (0, 0)),
        ),
        name="near",
    )(e_field, h_field, material, up_in, down_in, strip, cup_in, cdown_in, permittivity, conductivity)
    recv = lax.all_to_all(near.reshape(256, 8, 128), ALL, 0, 0, tiled=True)

    e_final, h_final = pl.pallas_call(
        yee_kernel,
        out_shape=(shape(*e_field.shape), shape(*h_field.shape)),
        in_specs=[vmem] * 8 + [smem, smem],
        out_specs=(vmem, vmem),
        scratch_shapes=[
            pltpu.VMEM((3, NZ + 1, 16, 256), F32),
            pltpu.VMEM((3, NZ + 1, 16, 256), F32),
            pltpu.VMEM((3, NZ, 16, 256), F32),
        ],
        cost_estimate=pl.CostEstimate(flops=40000000, transcendentals=0, bytes_accessed=8000000),
        name="yee",
    )(e_field, h_field, material, up_in, down_in, strip, cup_in, cdown_in, permittivity, conductivity)

    partial = pl.pallas_call(
        image_kernel,
        out_shape=shape(2 * GRID, 128),
        in_specs=[smem, smem] + [vmem] * 9,
        out_specs=vmem,
        scratch_shapes=[
            pltpu.VMEM((2 * K, 512), BF16),
            pltpu.VMEM((2, K, 128), F32),
            pltpu.VMEM((2, K, 128), F32),
            pltpu.VMEM((4, 256, 1024), BF16),
            pltpu.VMEM((GRID, 128), F32),
        ],
        name="image",
    )(
        info.astype(jnp.int32), info, recv.reshape(32, 8, 8, 128), tyh, tyl, txh, txl, second,
        first, upsample, pupil_mask,
    )
    pieces = lax.all_to_all(partial.reshape(256, 2, 128), ALL, 0, 0, tiled=True)
    image = pl.pallas_call(
        sum_kernel,
        out_shape=shape(2, IMG),
        in_specs=[vmem, vmem],
        out_specs=vmem,
        name="total",
    )(pieces.reshape(512, 128), upsample)
    return image, e_final, h_final


def solution(mesh):
    finer = Mesh(mesh.devices.reshape(4, 4, 2, 2, 4), ALL)
    return jax.shard_map(
        local,
        mesh=finer,
        in_specs=(
            P(None, None, GX, GY),
            P(None, None, GX, GY),
            P(None, GX, GY),
            P(),
            P(),
            P(ALL, None),
            P(ALL),
            P(),
        ),
        out_specs=(P(ALL, None), P(None, None, GX, GY), P(None, None, GX, GY)),
        check_vma=False,
    )
```

time: 492 us -> 118 us (0.24); the launches traced: 484 us -> 117 us
  waiting for transfers between devices: 136 us -> 26.3 us
  blocking collectives: 109 us -> 0 us
  local copies, waits for them, and re-layouts: 97.1 us -> 3.37 us
  other arithmetic: 79.5 us -> 0.6 us
  Pallas kernels: 0 us -> 37.1 us
  starting transfers between devices: 12.3 us -> 49.3 us
  matrix products: 31.4 us -> 0 us
  between operations: 17.4 us -> 0.77 us
    unnamed x6 -> x0, waiting for transfers between devices: 135 us -> none
    psum x1 -> x0, blocking collectives: 95.8 us -> none  [local(): spectrum_b = lax.psum(partial_value, GX_GY).astype(jnp.bfloat16)]
    pallas_call x0 -> x7, Pallas kernels: none -> 37.1 us  [the longest x1 14.7 us: local(): pl.pallas_call(yee_kernel, out_shape=(shape(*e_field.shape), shape(*h_fie...]
    dot_general x19 -> x0, matrix products: 31.4 us -> none  [the longest x16 25.8 us: add(): field = jnp.dot(rows, item[0], preferred_element_type=jnp.float32)]
    all_to_all x0 -> x2, starting transfers between devices: none -> 31.3 us  [the longest x1 24.7 us: local(): recv = lax.all_to_all(near.reshape(256, 8, 128), ALL, 0, 0, tiled=True)]
    add x25 -> x0, other arithmetic: 27 us -> none  [the longest x16 19.9 us: add(): total + item[1] * (field[:count] * field[:count] + field[count:] * field[...]
    slice x36 -> x0, local copies, waits for them, and re-layouts: 24.2 us -> none  [the longest x3 10.4 us: extended(): lax.slice_in_dim(block, block.shape[dim] - width, None, axis=dim)]
    gather x40 -> x0, local copies, waits for them, and re-layouts: 22.3 us -> none
  transfers between devices with their start and end apart: 7 -> 8, of which waited for: 4 -> 5; matrix products, arithmetic and copies ran while one was open for 7% -> 1% of each run, Pallas kernels for 0% -> 14%
where the time goes in v1:
time: 118 us; the launch traced here: 117 us
  starting transfers between devices  49.3 us (42%)
  Pallas kernels  37.1 us (31%)
  waiting for transfers between devices  26.3 us (22%)
  local copies, waits for them, and re-layouts  3.37 us (3%)
    all_to_all x1, starting transfers between devices, local(): recv = lax.all_to_all(near.reshape(256, 8, 128), ALL, 0, 0, tiled=True)  24.7 us
    all_to_all x1, waiting for transfers between devices, local(): recv = lax.all_to_all(near.reshape(256, 8, 128), ALL, 0, 0, tiled=True)  19.7 us
    ppermute x6, starting transfers between devices, shifted(): lax.ppermute(value, axes, [(i, i + by) for i in range(count) if 0 <= i +...  18 us
    pallas_call x1, Pallas kernels, local(): pl.pallas_call(yee_kernel, out_shape=(shape(*e_field.shape), shape(*h_fie...  14.7 us
    pallas_call x1, Pallas kernels, local(): pl.pallas_call(image_kernel, out_shape=shape(2 * GRID, 128), in_specs=[sm...  9.94 us
    all_to_all x1, starting transfers between devices, local(): pieces = lax.all_to_all(partial.reshape(256, 2, 128), ALL, 0, 0, tiled=True)  6.55 us
    ppermute x6, waiting for transfers between devices, shifted(): lax.ppermute(value, axes, [(i, i + by) for i in range(count) if 0 <= i +...  5.53 us
    unnamed x22, local copies, waits for them, and re-layouts  3.37 us
  transfers between devices with their start and end apart: 8, of which 5 were waited for; matrix products, arithmetic and copies ran while one was open for 1% of the time, Pallas kernels for 14%

profile of v1, /device:TPU:1, one launch (start us, length us, event | category | flops | bytes accessed | tf_op | source)
XLA Modules:
  0.0 117.4 jit_solution(3289056672201554326)
XLA Ops:
  0.6 3.0 %strip.1 = (f32[15,8,128]{2,1,0:T(8,128)}, f32[15,8,128]{2,1,0:T(8,128)}) custom-call(f32[3,64,8,128]{3,2,1,0:T(8,128)} %e_ref.7, f32[3,64,8,128]{3,2,1,0:T(8,128)} %h_ref.7, s32[64,8,128]{2,1,0:T(8,128)} %mat_ref.7, s32[2,8]{1,0:T(2,128)} %bitcast.9, f32[8]{0:T(128)} %weight_ref.1), custom_call_target="tpu_custom_call" | custom-call | tf_op jit(solution)/shard_map/strip/pallas_call | solution.py:398
  3.6 2.8 %rows.1 = (f32[7,32,8,128]{3,2,1,0:T(8,128)}, f32[7,32,8,128]{3,2,1,0:T(8,128)}) custom-call(f32[3,64,8,128]{3,2,1,0:T(8,128)} %e_ref.7, f32[3,64,8,128]{3,2,1,0:T(8,128)} %h_ref.7, s32[64,8,128]{2,1,0:T(8,128)} %mat_ref.7, f32[15,8,128]{2,1,0:T(8,128)} %get-tuple-element.14.after_ref.own_ref), custom_call_target="tpu_custom_call" | custom-call | tf_op jit(solution)/shard_map/rows/pallas_call | solution.py:407
  6.4 4.6 %collective-permute-start = (f32[7,32,8,128]{3,2,1,0:T(8,128)}, f32[7,32,8,128]{3,2,1,0:T(8,128)S(1)}, u32[]{:S(2)}, u32[]{:S(2)}) collective-permute-start(f32[7,32,8,128]{3,2,1,0:T(8,128)} %get-tuple-element.15), channel_id=1, source_target_pairs={{0,8},{8,16},{16,24},{24,32},{32,40},{40,48},{48,56},{56,64},{64,7... | collective-permute-start | bytes 2752520 | tf_op jit(solution)/shard_map/ppermute | solution.py:383
  11.0 1.9 %collective-permute-start.1 = (f32[7,32,8,128]{3,2,1,0:T(8,128)}, f32[7,32,8,128]{3,2,1,0:T(8,128)S(1)}, u32[]{:S(2)}, u32[]{:S(2)}) collective-permute-start(f32[7,32,8,128]{3,2,1,0:T(8,128)} %get-tuple-element.16), channel_id=1, source_target_pairs={{8,0},{16,8},{24,16},{32,24},{40,32},{48,40},{56,48},{64,56},{72,6... | collective-permute-start | bytes 2752520 | tf_op jit(solution)/shard_map/ppermute | solution.py:383
  12.9 1.3 %collective-permute-start.3 = (f32[15,8,128]{2,1,0:T(8,128)S(1)}, f32[15,8,128]{2,1,0:T(8,128)S(1)}, u32[]{:S(2)}, u32[]{:S(2)}) collective-permute-start(f32[15,8,128]{2,1,0:T(8,128)S(1)} %copy-done.6), channel_id=1, source_target_pairs={{1,0},{2,1},{3,2},{4,3},{5,4},{6,5},{7,6},{9,8},{10,9},{11,10},{12... | collective-permute-start | bytes 184328 | tf_op jit(solution)/shard_map/ppermute | solution.py:383
  14.2 4.0 %collective-permute-start.2 = (f32[15,8,128]{2,1,0:T(8,128)S(1)}, f32[15,8,128]{2,1,0:T(8,128)S(1)}, u32[]{:S(2)}, u32[]{:S(2)}) collective-permute-start(f32[15,8,128]{2,1,0:T(8,128)S(1)} %copy-done.10), channel_id=1, source_target_pairs={{0,1},{1,2},{2,3},{3,4},{4,5},{5,6},{6,7},{8,9},{9,10},{10,11},{11... | collective-permute-start | bytes 184328 | tf_op jit(solution)/shard_map/ppermute | solution.py:383
  18.4 1.5 %collective-permute-done.2.low_ref = f32[15,8,128]{2,1,0:T(8,128)S(1)} collective-permute-done((f32[15,8,128]{2,1,0:T(8,128)S(1)}, f32[15,8,128]{2,1,0:T(8,128)S(1)}, u32[]{:S(2)}, u32[]{:S(2)}) %collective-permute-start.2) | collective-permute-done | bytes 61472 | tf_op jit(solution)/shard_map/ppermute | solution.py:383
  20.0 0.6 copy-done.8
  20.6 1.7 %corner.1 = (f32[29,8,128]{2,1,0:T(8,128)}, f32[15,8,128]{2,1,0:T(8,128)}, f32[15,8,128]{2,1,0:T(8,128)}) custom-call(f32[15,8,128]{2,1,0:T(8,128)} %copy-done.8, f32[15,8,128]{2,1,0:T(8,128)} %copy-done.7, f32[15,8,128]{2,1,0:T(8,128)} %get-tuple-element.14.after_ref.own_ref), custom_call_target="tpu_custom_call" | custom-call | tf_op jit(solution)/shard_map/corner/pallas_call | solution.py:416
  22.3 4.3 %collective-permute-start.4 = (f32[15,8,128]{2,1,0:T(8,128)}, f32[15,8,128]{2,1,0:T(8,128)S(1)}, u32[]{:S(2)}, u32[]{:S(2)}) collective-permute-start(f32[15,8,128]{2,1,0:T(8,128)} %get-tuple-element.19), channel_id=1, source_target_pairs={{0,8},{8,16},{16,24},{24,32},{32,40},{40,48},{48,56},{56,64},{64,7... | collective-permute-start | bytes 184328 | tf_op jit(solution)/shard_map/ppermute | solution.py:383
  26.6 1.9 %collective-permute-start.5 = (f32[15,8,128]{2,1,0:T(8,128)}, f32[15,8,128]{2,1,0:T(8,128)S(1)}, u32[]{:S(2)}, u32[]{:S(2)}) collective-permute-start(f32[15,8,128]{2,1,0:T(8,128)} %get-tuple-element.20), channel_id=1, source_target_pairs={{8,0},{16,8},{24,16},{32,24},{40,32},{48,40},{56,48},{64,56},{72,6... | collective-permute-start | bytes 184328 | tf_op jit(solution)/shard_map/ppermute | solution.py:383
  28.5 3.8 %collective-permute-done.5.cdown_ref = f32[15,8,128]{2,1,0:T(8,128)S(1)} collective-permute-done((f32[15,8,128]{2,1,0:T(8,128)}, f32[15,8,128]{2,1,0:T(8,128)S(1)}, u32[]{:S(2)}, u32[]{:S(2)}) %collective-permute-start.5) | collective-permute-done | bytes 61472 | tf_op jit(solution)/shard_map/ppermute | solution.py:383
  32.4 0.6 copy-done.5
  33.6 2.7 %near.1 = (bf16[16,2,8,8,128]{4,3,2,1,0:T(8,128)(2,1)}, f32[8,128]{1,0:T(8,128)}) custom-call(f32[3,64,8,128]{3,2,1,0:T(8,128)} %e_ref.7, f32[3,64,8,128]{3,2,1,0:T(8,128)} %h_ref.7, s32[64,8,128]{2,1,0:T(8,128)} %mat_ref.7, f32[7,32,8,128]{3,2,1,0:T(8,128)} %copy-done, f32[7,32,8,128]{3,2,1,0:T(8,128)} %copy-done.1, ...), custom_call_target="tpu_custom_call" | custom-call | tf_op jit(solution)/shard_map/near/pallas_call | solution.py:428
  36.4 24.7 %all-to-all-start = ((bf16[256,8,128]{2,1,0:T(8,128)(2,1)}), bf16[256,8,128]{2,1,0:T(8,128)(2,1)S(1)}, u32[]{:S(2)}, u32[]{:S(2)}) async-start(bf16[256,8,128]{2,1,0:T(8,128)(2,1)} %bitcast.8), calls=%async_computation | async-start | bytes 1048576 | tf_op jit(solution)/shard_map/all_to_all | solution.py:444
  61.1 0.6 convert_element_type.3.place_ref
  61.7 19.7 %all-to-all-done = bf16[256,8,128]{2,1,0:T(8,128)(2,1)S(1)} async-done(((bf16[256,8,128]{2,1,0:T(8,128)(2,1)}), bf16[256,8,128]{2,1,0:T(8,128)(2,1)S(1)}, u32[]{:S(2)}, u32[]{:S(2)}) %all-to-all-start) | async-done | bytes 524320 | tf_op jit(solution)/shard_map/all_to_all | solution.py:444
  81.4 0.8 copy-done.2
  82.2 9.9 %image.1 = f32[512,128]{1,0:T(8,128)} custom-call(s32[8,128]{1,0:T(8,128)} %convert_element_type.3.place_ref, f32[8,128]{1,0:T(8,128)} %get-tuple-element.21.info_ref, bf16[32,8,8,128]{3,2,1,0:T(8,128)(2,1)} %bitcast.5, bf16[512,512]{1,0:T(8,128)(2,1)} %constant.14.clone.tyh_ref, bf16[512,512]{1,0:T(8,128)(2,1)} %constant.15.clone.tyl_ref, ...), custom_call_target="tpu_custom_call" | custom-call | tf_op jit(solution)/shard_map/image/pallas_call | solution.py:460
  92.2 6.5 %all-to-all-start.1 = ((f32[256,2,128]{2,1,0:T(2,128)}), f32[256,2,128]{2,1,0:T(2,128)S(1)}, u32[]{:S(2)}, u32[]{:S(2)}) async-start(f32[256,2,128]{2,1,0:T(2,128)} %bitcast.7), calls=%async_computation.1 | async-start | bytes 524288 | tf_op jit(solution)/shard_map/all_to_all | solution.py:477
  98.7 14.7 %yee.1 = (f32[3,64,8,128]{3,2,1,0:T(8,128)}, f32[3,64,8,128]{3,2,1,0:T(8,128)}) custom-call(f32[3,64,8,128]{3,2,1,0:T(8,128)} %e_ref.7, f32[3,64,8,128]{3,2,1,0:T(8,128)} %h_ref.7, s32[64,8,128]{2,1,0:T(8,128)} %mat_ref.7, f32[7,32,8,128]{3,2,1,0:T(8,128)} %copy-done, f32[7,32,8,128]{3,2,1,0:T(8,128)} %copy-done.1, ...), custom_call_target="tpu_custom_call" | custom-call | flops 40000000 | bytes 8000000 | tf_op jit(solution)/shard_map/yee/pallas_call | solution.py:446
  113.4 1.1 all-to-all-done.1
  114.4 0.7 copy-done.3
  115.1 2.3 %total.1 = f32[2,512]{1,0:T(2,128)} custom-call(f32[512,128]{1,0:T(8,128)} %bitcast.6, f32[512,256]{1,0:T(8,128)} %constant.20.clone.up_ref), custom_call_target="tpu_custom_call" | custom-call | tf_op jit(solution)/shard_map/total/pallas_call | solution.py:478
  (22 shorter events, 0.9 us)
Async XLA Ops:
  3.6 9.3 %copy-start.6 = (f32[15,8,128]{2,1,0:T(8,128)S(1)}, f32[15,8,128]{2,1,0:T(8,128)}, u32[]{:S(2)}) copy-start(f32[15,8,128]{2,1,0:T(8,128)} %get-tuple-element.14.after_ref.own_ref) | copy-start | bytes 184324
  3.6 10.6 %copy-start.10 = (f32[15,8,128]{2,1,0:T(8,128)S(1)}, f32[15,8,128]{2,1,0:T(8,128)}, u32[]{:S(2)}) copy-start(f32[15,8,128]{2,1,0:T(8,128)} %get-tuple-element.17) | copy-start | bytes 184324
  6.4 25.9 %collective-permute-start = (f32[7,32,8,128]{3,2,1,0:T(8,128)}, f32[7,32,8,128]{3,2,1,0:T(8,128)S(1)}, u32[]{:S(2)}, u32[]{:S(2)}) collective-permute-start(f32[7,32,8,128]{3,2,1,0:T(8,128)} %get-tuple-element.15), channel_id=1, source_target_pairs={{0,8},{8,16},{16,24},{24,32},{32,40},{40,48},{48,56},{56,64},{64,7... | collective-permute-start | bytes 2752520 | tf_op jit(solution)/shard_map/ppermute | solution.py:383
  11.0 21.4 %collective-permute-start.1 = (f32[7,32,8,128]{3,2,1,0:T(8,128)}, f32[7,32,8,128]{3,2,1,0:T(8,128)S(1)}, u32[]{:S(2)}, u32[]{:S(2)}) collective-permute-start(f32[7,32,8,128]{3,2,1,0:T(8,128)} %get-tuple-element.16), channel_id=1, source_target_pairs={{8,0},{16,8},{24,16},{32,24},{40,32},{48,40},{56,48},{64,56},{72,6... | collective-permute-start | bytes 2752520 | tf_op jit(solution)/shard_map/ppermute | solution.py:383
  12.9 5.5 %collective-permute-start.3 = (f32[15,8,128]{2,1,0:T(8,128)S(1)}, f32[15,8,128]{2,1,0:T(8,128)S(1)}, u32[]{:S(2)}, u32[]{:S(2)}) collective-permute-start(f32[15,8,128]{2,1,0:T(8,128)S(1)} %copy-done.6), channel_id=1, source_target_pairs={{1,0},{2,1},{3,2},{4,3},{5,4},{6,5},{7,6},{9,8},{10,9},{11,10},{12... | collective-permute-start | bytes 184328 | tf_op jit(solution)/shard_map/ppermute | solution.py:383
  14.2 5.7 %collective-permute-start.2 = (f32[15,8,128]{2,1,0:T(8,128)S(1)}, f32[15,8,128]{2,1,0:T(8,128)S(1)}, u32[]{:S(2)}, u32[]{:S(2)}) collective-permute-start(f32[15,8,128]{2,1,0:T(8,128)S(1)} %copy-done.10), channel_id=1, source_target_pairs={{0,1},{1,2},{2,3},{3,4},{4,5},{5,6},{6,7},{8,9},{9,10},{10,11},{11... | collective-permute-start | bytes 184328 | tf_op jit(solution)/shard_map/ppermute | solution.py:383
  18.4 1.5 %copy-start.7 = (f32[15,8,128]{2,1,0:T(8,128)}, f32[15,8,128]{2,1,0:T(8,128)S(1)}, u32[]{:S(2)}) copy-start(f32[15,8,128]{2,1,0:T(8,128)S(1)} %collective-permute-done.3.high_ref) | copy-start | bytes 184324
  20.0 0.6 copy-start.8
  22.3 6.3 %collective-permute-start.4 = (f32[15,8,128]{2,1,0:T(8,128)}, f32[15,8,128]{2,1,0:T(8,128)S(1)}, u32[]{:S(2)}, u32[]{:S(2)}) collective-permute-start(f32[15,8,128]{2,1,0:T(8,128)} %get-tuple-element.19), channel_id=1, source_target_pairs={{0,8},{8,16},{16,24},{24,32},{32,40},{40,48},{48,56},{56,64},{64,7... | collective-permute-start | bytes 184328 | tf_op jit(solution)/shard_map/ppermute | solution.py:383
  26.6 5.8 %collective-permute-start.5 = (f32[15,8,128]{2,1,0:T(8,128)}, f32[15,8,128]{2,1,0:T(8,128)S(1)}, u32[]{:S(2)}, u32[]{:S(2)}) collective-permute-start(f32[15,8,128]{2,1,0:T(8,128)} %get-tuple-element.20), channel_id=1, source_target_pairs={{8,0},{16,8},{24,16},{32,24},{40,32},{48,40},{56,48},{64,56},{72,6... | collective-permute-start | bytes 184328 | tf_op jit(solution)/shard_map/ppermute | solution.py:383
  28.5 3.8 %copy-start.4 = (f32[15,8,128]{2,1,0:T(8,128)}, f32[15,8,128]{2,1,0:T(8,128)S(1)}, u32[]{:S(2)}) copy-start(f32[15,8,128]{2,1,0:T(8,128)S(1)} %collective-permute-done.4.cup_ref) | copy-start | bytes 184324
  32.4 0.6 copy-start.5
  32.4 1.0 copy-start
  32.4 1.3 %copy-start.1 = (f32[7,32,8,128]{3,2,1,0:T(8,128)}, f32[7,32,8,128]{3,2,1,0:T(8,128)S(1)}, u32[]{:S(2)}) copy-start(f32[7,32,8,128]{3,2,1,0:T(8,128)S(1)} %collective-permute-done.1.down_ref) | copy-start | bytes 2752516
  36.4 24.7 %copy-start.9 = (f32[8,128]{1,0:T(8,128)S(1)}, f32[8,128]{1,0:T(8,128)}, u32[]{:S(2)}) copy-start(f32[8,128]{1,0:T(8,128)} %get-tuple-element.21.info_ref) | copy-start | bytes 12292
  36.4 45.1 %all-to-all-start = ((bf16[256,8,128]{2,1,0:T(8,128)(2,1)}), bf16[256,8,128]{2,1,0:T(8,128)(2,1)S(1)}, u32[]{:S(2)}, u32[]{:S(2)}) async-start(bf16[256,8,128]{2,1,0:T(8,128)(2,1)} %bitcast.8), calls=%async_computation | async-start | bytes 1048576 | tf_op jit(solution)/shard_map/all_to_all | solution.py:444
  81.4 0.8 copy-start.2
  92.2 22.3 %all-to-all-start.1 = ((f32[256,2,128]{2,1,0:T(2,128)}), f32[256,2,128]{2,1,0:T(2,128)S(1)}, u32[]{:S(2)}, u32[]{:S(2)}) async-start(f32[256,2,128]{2,1,0:T(2,128)} %bitcast.7), calls=%async_computation.1 | async-start | bytes 524288 | tf_op jit(solution)/shard_map/all_to_all | solution.py:477
  114.4 0.7 copy-start.3

commit v2 on v1

--- a/solution.py
+++ b/solution.py
@@ -6,6 +6,7 @@
 from jax.experimental.pallas import tpu as pltpu
 from jax.sharding import Mesh
 from jax.sharding import PartitionSpec as P
+
 
 STEPS = 4
 COURANT = 0.5
@@ -17,7 +18,8 @@
 MATS = 8
 SOURCES = 2048
 TOP = 5
-BLOCK = 8
+BLOCK = 16
+THIN = 36
 GX = ("zl", "y", "c")
 GY = ("zh", "x")
 ALL = GX + GY
@@ -33,9 +35,9 @@
 
 def tables(rows_all, cols_all):
     freqs = np.arange(K) - K // 2
-    phase_y = 2.0 * np.pi * (np.outer(np.arange(cols_all // 2), freqs) % cols_all) / cols_all
+    phase_y = 2.0 * np.pi * (np.outer(np.arange(cols_all // 2) + STEPS, freqs) % cols_all) / cols_all
     ty = np.concatenate((np.cos(phase_y), -np.sin(phase_y)), axis=1)
-    phase_x = 2.0 * np.pi * (np.outer(freqs, np.arange(rows_all)) % rows_all) / rows_all
+    phase_x = 2.0 * np.pi * (np.outer(freqs, np.arange(rows_all) + STEPS) % rows_all) / rows_all
     tx = np.concatenate((np.cos(phase_x), np.sin(phase_x)), axis=0)
     offsets = np.arange(PW) - PW // 2
     places = 2 * np.arange(GRID)
@@ -89,17 +91,36 @@
     return (mat_ref[...] + 1).astype(F32)
 
 
-def strip_kernel(e_ref, h_ref, mat_ref, shift_ref, weight_ref, low_ref, high_ref):
+def thin_component(e_ref, h_ref, mat_ref, comp, z):
+    if comp < 3:
+        return e_ref[comp, z]
+    if comp < 6:
+        return h_ref[comp - 3, z]
+    return (mat_ref[z] + 1).astype(F32)
+
+
+def packed_strip(block):
     slot = (lane_iota((4, 8, 128)) + 4) // 8 % 16
-    first = lane_iota((2, 8, 128)) % 8 < 4
+    layers = block.reshape(4, 16, 8, 128)
+    strip = layers[:, 0]
+    for s in range(1, 16):
+        strip = jnp.where(slot == s, pltpu.roll(layers[:, s], 8 * s, axis=2), strip)
+    return strip[:2], pltpu.roll(strip[2:], 4, axis=2)
+
+
+def thin_kernel(e_ref, h_ref, mat_ref, shift_ref, weight_ref, down_ref, low_ref):
+    slot = lane_iota((8, 128)) // 8
+    thin = []
     for comp in range(7):
-        layers = component(e_ref, h_ref, mat_ref, comp).reshape(4, 16, 8, 128)
-        strip = layers[:, 0]
-        for s in range(1, 16):
-            strip = jnp.where(slot == s, pltpu.roll(layers[:, s], 8 * s, axis=2), strip)
-        turned = pltpu.roll(strip[2:], 4, axis=2)
-        low_ref[pl.ds(2 * comp, 2)] = jnp.where(first, strip[:2], turned)
-        high_ref[pl.ds(2 * comp, 2)] = jnp.where(first, turned, strip[:2])
+        for z in range(8 - TOP, 8):
+            thin.append(thin_component(e_ref, h_ref, mat_ref, comp, z))
+    for k, tile in enumerate(thin):
+        down_ref[k] = tile
+    for g in range(3):
+        strip = thin[16 * g]
+        for s, tile in enumerate(thin[16 * g + 1 : 16 * g + 16]):
+            strip = jnp.where(slot == s + 1, pltpu.roll(tile, 8 * (s + 1), axis=1), strip)
+        low_ref[g] = strip
     row = sub_iota((8, 128))
     lane = lane_iota((8, 128))
     info = jnp.zeros((8, 128), F32)
@@ -108,23 +129,40 @@
         info = jnp.where(here & (lane == 0), shift_ref[0, s].astype(F32), info)
         info = jnp.where(here & (lane == 1), shift_ref[1, s].astype(F32), info)
         info = jnp.where(here & (lane == 2), weight_ref[s], info)
-    low_ref[14] = info
-    high_ref[14] = info
+    down_ref[THIN - 1] = info
+    low_ref[3] = info
+
+
+def strip_kernel(e_ref, h_ref, mat_ref, after_ref, low_ref, high_ref):
+    first = lane_iota((2, 8, 128)) % 8 < 4
+    for comp in range(7):
+        near, far = packed_strip(component(e_ref, h_ref, mat_ref, comp))
+        low_ref[pl.ds(2 * comp, 2)] = jnp.where(first, near, far)
+        high_ref[pl.ds(2 * comp, 2)] = jnp.where(first, far, near)
 
 
 def rows_kernel(e_ref, h_ref, mat_ref, after_ref, up_ref, down_ref):
     for comp in range(7):
         block = component(e_ref, h_ref, mat_ref, comp)
         up, down = pair_rows(block[:32], block[32:])
-        up_ref[comp] = up
-        down_ref[comp] = down
-
-
-def corner_kernel(low_ref, high_ref, own_ref, strip_ref, up_ref, down_ref):
+        up_ref[pl.ds(32 * comp, 32)] = up
+        down_ref[pl.ds(32 * comp, 32)] = down
+
+
+def at_end(axes, last):
+    flag = None
+    for axis in axes:
+        here = lax.axis_index(axis) == (lax.axis_size(axis) - 1 if last else 0)
+        flag = here if flag is None else flag & here
+    return flag
+
+
+def corner_kernel(low_ref, high_ref, strip_ref, up_ref, down_ref):
     first = lane_iota((2, 8, 128)) % 8 < 4
+    no_low, no_high = at_end(GY, False), at_end(GY, True)
     for comp in range(7):
-        low = low_ref[pl.ds(2 * comp, 2)]
-        high = high_ref[pl.ds(2 * comp, 2)]
+        low = jnp.where(no_low, 0.0, low_ref[pl.ds(2 * comp, 2)])
+        high = jnp.where(no_high, 0.0, high_ref[pl.ds(2 * comp, 2)])
         near = jnp.where(first, high, low)
         far = pltpu.roll(jnp.where(first, low, high), 124, axis=2)
         strip_ref[pl.ds(4 * comp, 2)] = near
@@ -132,26 +170,26 @@
         up, down = pair_rows(near, far)
         up_ref[pl.ds(2 * comp, 2)] = up
         down_ref[pl.ds(2 * comp, 2)] = down
-    odd = lax.axis_index("x") % 2 == 1
-    other = jnp.where(odd, low_ref[14], high_ref[14])
-    info = jnp.where(lane_iota((8, 128)) < 8, own_ref[14], pltpu.roll(other, 8, axis=1))
-    strip_ref[28] = info
-    up_ref[14] = info
-    down_ref[14] = info
-
-
-def lookup(code, eps_ref, sig_ref):
-    keep = jnp.zeros(code.shape, F32)
-    drive = jnp.zeros(code.shape, F32)
-    one = jnp.ones((8, 128), F32)
+
+
+def table_of(eps_ref, sig_ref):
+    keeps, drives = [], []
+    one = jnp.ones((1, 256), F32)
     for index in range(MATS):
         eps = one * eps_ref[index]
         loss = (one * sig_ref[index]) / (2.0 * eps)
-        keep_one = ((1.0 - loss) / (1.0 + loss))[:1, :1]
-        drive_one = (COURANT / (eps * (1.0 + loss)))[:1, :1]
+        keeps.append((1.0 - loss) / (1.0 + loss))
+        drives.append(COURANT / (eps * (1.0 + loss)))
+    return keeps, drives
+
+
+def lookup(code, table):
+    keep = jnp.zeros(code.shape, F32)
+    drive = jnp.zeros(code.shape, F32)
+    for index in range(MATS):
         chosen = code == index + 1.0
-        keep = jnp.where(chosen, keep_one, keep)
-        drive = jnp.where(chosen, drive_one, drive)
+        keep = jnp.where(chosen, table[0][index], keep)
+        drive = jnp.where(chosen, table[1][index], drive)
     return keep, drive
 
 
@@ -173,12 +211,12 @@
     return pltpu.roll(field, 1, axis=axis)
 
 
-def magnetic(e, e_next, h, inside):
+def magnetic(e, e_next, h, rate):
     ex, ey, ez = e
-    new_x = h[0] - COURANT * (ahead(ez, 1) - ez - (e_next[1] - ey))
-    new_y = h[1] - COURANT * (e_next[0] - ex - (ahead(ez, 0) - ez))
-    new_z = h[2] - COURANT * (ahead(ey, 0) - ey - (ahead(ex, 1) - ex))
-    return new_x * inside, new_y * inside, new_z * inside
+    new_x = h[0] - rate * (ahead(ez, 1) - ez - (e_next[1] - ey))
+    new_y = h[1] - rate * (e_next[0] - ex - (ahead(ez, 0) - ez))
+    new_z = h[2] - rate * (ahead(ey, 0) - ey - (ahead(ex, 1) - ex))
+    return new_x, new_y, new_z
 
 
 def electric(e, h, h_last, keep, drive):
@@ -190,46 +228,65 @@
 
 
 def near_kernel(
-    e_ref, h_ref, mat_ref, up_ref, down_ref, strip_ref, cup_ref, cdown_ref, eps_ref, sig_ref,
-    near_ref, info_ref,
+    own_ref, down_ref, high_ref, corner_ref, eps_ref, sig_ref, near_ref, info_ref
 ):
     fields = []
     for comp in range(7):
-        _, far = unpair_rows(up_ref[comp], down_ref[comp])
-        _, corner = unpair_rows(cup_ref[2 * comp + 1], cdown_ref[2 * comp + 1])
-        strip = strip_ref[4 * comp + 3]
         layers = []
-        for z in range(8 - TOP, 8):
-            if comp < 3:
-                own = e_ref[comp, z]
-            elif comp < 6:
-                own = h_ref[comp - 3, z]
-            else:
-                own = (mat_ref[z] + 1).astype(F32)
-            layers.append(wide(own, far[z], strip, corner, 8 + z))
+        for z in range(TOP):
+            k = comp * TOP + z
+            group, slot = divmod(k, 16)
+            layers.append(
+                wide(own_ref[k], down_ref[k], high_ref[group], corner_ref[group], slot)
+            )
         fields.append(layers)
     e = [tuple(fields[c][z] for c in range(3)) for z in range(TOP)]
     h = [tuple(fields[c + 3][z] for c in range(3)) for z in range(TOP)]
     zero = jnp.zeros((16, 256), F32)
-    coefs = []
-    for z in range(TOP):
-        code = fields[6][z]
-        coefs.append(lookup(code, eps_ref, sig_ref) + ((code > 0.5).astype(F32),))
+    table = table_of(eps_ref, sig_ref)
+    coefs = [lookup(fields[6][z], table) for z in range(TOP)]
+    last_x, last_y = at_end(GX, True), at_end(GY, True)
+    row, lane = sub_iota((16, 256)), lane_iota((16, 256))
+
+    def kept(flag, place, at):
+        return 1.0 - (place == at).astype(F32) * flag.astype(F32)
+
+    masks = {
+        (0, 1): kept(last_x, row, 7), (1, 1): kept(last_y, lane, 127),
+        (0, 0): kept(last_x, row, 8), (1, 0): kept(last_y, lane, 128),
+    }
+
+    def over(field, axis):
+        return ahead(field, axis) * masks[axis, 1]
+
+    def back(field, axis):
+        return behind(field, axis) * masks[axis, 0]
+
     for step in range(STEPS):
         for z in range(step, TOP):
-            keep, drive, inside = coefs[z]
+            ex, ey, ez = e[z]
             e_next = e[z + 1] if z + 1 < TOP else (zero, zero)
-            h[z] = magnetic(e[z], e_next, h[z], inside)
-            if z > step:
-                e[z] = electric(e[z], h[z], h[z - 1], keep, drive)
+            h[z] = (
+                h[z][0] - COURANT * (over(ez, 1) - ez - (e_next[1] - ey)),
+                h[z][1] - COURANT * (e_next[0] - ex - (over(ez, 0) - ez)),
+                h[z][2] - COURANT * (over(ey, 0) - ey - (over(ex, 1) - ex)),
+            )
+        for z in range(step + 1, TOP):
+            keep, drive = coefs[z]
+            hx, hy, hz = h[z]
+            e[z] = (
+                keep * e[z][0] + drive * (hz - back(hz, 1) - (hy - h[z - 1][1])),
+                keep * e[z][1] + drive * (hx - h[z - 1][0] - (hz - back(hz, 0))),
+                keep * e[z][2] + drive * (hy - back(hy, 0) - (hx - back(hx, 1))),
+            )
     for pol in range(2):
-        tile = e[TOP - 1][pol][:8, :128].astype(BF16)
-        near_ref[:, pol] = jnp.broadcast_to(tile, (16, 8, 8, 128))
-    up = lax.axis_index("c") == 1
-    other = jnp.where(up, cup_ref[14], cdown_ref[14])
-    info_ref[...] = jnp.where(
-        lane_iota((8, 128)) < 16, strip_ref[28], pltpu.roll(other, 16, axis=1)
-    )
+        tile = pltpu.roll(pltpu.roll(e[TOP - 1][pol], 12, axis=0), 252, axis=1)
+        near_ref[:, pol] = jnp.broadcast_to(tile[:8, :128].astype(BF16), (16, 8, 8, 128))
+    lane = lane_iota((8, 128))
+    info = own_ref[THIN - 1]
+    for k, other in enumerate((high_ref[3], down_ref[THIN - 1], corner_ref[3])):
+        info = jnp.where(lane < 8 * k + 8, info, pltpu.roll(other, 8 * k + 8, axis=1))
+    info_ref[...] = info
 
 
 def yee_kernel(
@@ -239,22 +296,23 @@
     for comp in range(3):
         e_s[comp, NZ] = jnp.zeros((16, 256), F32)
         h_s[comp, 0] = jnp.zeros((16, 256), F32)
+    no_up, no_down = at_end(GX, False), at_end(GX, True)
     for comp in range(7):
-        near, far = unpair_rows(up_ref[comp], down_ref[comp])
-        c_near, c_far = unpair_rows(
-            cup_ref[pl.ds(2 * comp, 2)], cdown_ref[pl.ds(2 * comp, 2)]
+        near, far = unpair_rows(
+            jnp.where(no_up, 0.0, up_ref[pl.ds(32 * comp, 32)]),
+            jnp.where(no_down, 0.0, down_ref[pl.ds(32 * comp, 32)]),
+        )
+        edge = unpair_rows(
+            jnp.where(no_up, 0.0, cup_ref[pl.ds(2 * comp, 2)]),
+            jnp.where(no_down, 0.0, cdown_ref[pl.ds(2 * comp, 2)]),
         )
         for z in range(NZ):
             group, slot = divmod(z, 16)
             rows = near[z] if z < 32 else far[z - 32]
-            corner = c_near[group] if group < 2 else c_far[group - 2]
-            if comp < 3:
-                own = e_ref[comp, z]
-            elif comp < 6:
-                own = h_ref[comp - 3, z]
-            else:
-                own = (mat_ref[z] + 1).astype(F32)
-            value = wide(own, rows, strip_ref[4 * comp + group], corner, slot)
+            own = thin_component(e_ref, h_ref, mat_ref, comp, z)
+            value = wide(
+                own, rows, strip_ref[4 * comp + group], edge[group // 2][group % 2], slot
+            )
             if comp < 3:
                 e_s[comp, z] = value
             elif comp < 6:
@@ -262,15 +320,19 @@
             else:
                 c_s[2, z] = value
 
-    def coef(z, carry):
-        code = c_s[2, z]
-        keep, drive = lookup(code, eps_ref, sig_ref)
-        c_s[0, z] = keep
-        c_s[1, z] = drive
-        c_s[2, z] = (code > 0.5).astype(F32)
+    table = table_of(eps_ref, sig_ref)
+
+    def coef(i, carry):
+        for j in range(4):
+            z = 4 * i + j
+            code = c_s[2, z]
+            keep, drive = lookup(code, table)
+            c_s[0, z] = keep
+            c_s[1, z] = drive
+            c_s[2, z] = jnp.where(code > 0.5, COURANT, 0.0)
         return carry
 
-    lax.fori_loop(0, NZ, coef, 0)
+    lax.fori_loop(0, NZ // 4, coef, 0)
 
     def step(k, carry):
         def block(i, carry):
@@ -314,7 +376,7 @@
 
 def image_kernel(
     place_ref, info_ref, recv_ref, tyh_ref, tyl_ref, txh_ref, txl_ref, second_ref, first_ref,
-    up_ref, mask_ref, out_ref, near_s, re_s, im_s, half_s, acc_s,
+    up_ref, mask_ref, after_ref, out_ref, near_s, re_s, im_s, half_s, acc_s,
 ):
     for j in range(8):
         tile = recv_ref[:, j].astype(F32).reshape(K, 128)
@@ -378,9 +440,22 @@
     out_ref[...] = full[:2]
 
 
-def shifted(value, axes, by):
+def shifted(value, axes, by, cyclic=True):
     count = lax.axis_size(axes)
-    return lax.ppermute(value, axes, [(i, i + by) for i in range(count) if 0 <= i + by < count])
+    pairs = [(i, (i + by) % count) for i in range(count)]
+    if not cyclic:
+        pairs = [(i, j) for i, j in pairs if j == i + by]
+    return lax.ppermute(value, axes, pairs)
+
+
+def diagonal(value):
+    rows, cols = lax.axis_size(GX), lax.axis_size(GY)
+    pairs = [
+        (i * cols + j, (i - 1) % rows * cols + (j - 1) % cols)
+        for i in range(rows)
+        for j in range(cols)
+    ]
+    return lax.ppermute(value, ALL, pairs)
 
 
 def local(
@@ -388,60 +463,80 @@
 ):
     rows_all = e_field.shape[2] * lax.axis_size(GX)
     cols_all = e_field.shape[3] * lax.axis_size(GY)
-    tyh, tyl, txh, txl, second, first, upsample = tables(rows_all, cols_all)
+    tyh, tyl, txh, txl, second, first, upsample = map(jnp.asarray, tables(rows_all, cols_all))
     smem = pl.BlockSpec(memory_space=pltpu.SMEM)
     vmem = pl.BlockSpec(memory_space=pltpu.VMEM)
 
+    params = pltpu.CompilerParams(vmem_limit_bytes=28 * 1024 * 1024)
+
+    def here(value):
+        return pltpu.with_memory_space_constraint(value, pltpu.VMEM)
+
+    def far(value):
+        return pltpu.with_memory_space_constraint(value, pltpu.HBM)
+
     def shape(*dims, dtype=F32):
         return jax.ShapeDtypeStruct(dims, dtype)
 
+    field = pl.BlockSpec((3, 8, 8, 128), lambda i: (0, 7, 0, 0))
+    layer = pl.BlockSpec((8, 8, 128), lambda i: (7, 0, 0))
+    thin = pl.BlockSpec((THIN, 8, 128), lambda i: (0, 0, 0))
+    head = pl.BlockSpec((4, 8, 128), lambda i: (0, 0, 0))
+    thin_x, thin_y = pl.pallas_call(
+        thin_kernel,
+        grid=(1,),
+        out_shape=(shape(THIN, 8, 128), shape(4, 8, 128)),
+        in_specs=[field, field, layer, smem, smem],
+        out_specs=(thin, head),
+        compiler_params=params,
+        name="thin",
+    )(far(e_field), far(h_field), far(material), src_shift.T, src_weight)
+    next_xy = diagonal(thin_y)
+    next_y = shifted(thin_y, GY, -1)
+    next_x = shifted(thin_x, GX, -1)
+    near, info = pl.pallas_call(
+        near_kernel,
+        out_shape=(shape(16, 2, 8, 8, 128, dtype=BF16), shape(8, 128)),
+        in_specs=[vmem] * 4 + [smem, smem],
+        out_specs=(vmem, vmem),
+        compiler_params=params,
+        name="near",
+    )(
+        here(thin_x), here(next_x), here(next_y), here(next_xy), permittivity, conductivity
+    )
+    recv = lax.all_to_all(near.reshape(256, 8, 128), ALL, 0, 0, tiled=True)
+
+    whole = [vmem, vmem, vmem, pl.BlockSpec(memory_space=pl.ANY)]
     to_low, to_high = pl.pallas_call(
         strip_kernel,
-        out_shape=(shape(15, 8, 128), shape(15, 8, 128)),
-        in_specs=[vmem, vmem, vmem, smem, smem],
+        out_shape=(shape(14, 8, 128), shape(14, 8, 128)),
+        in_specs=whole,
         out_specs=(vmem, vmem),
+        compiler_params=params,
         name="strip",
-    )(e_field, h_field, material, src_shift.T, src_weight)
+    )(e_field, h_field, material, thin_y)
     low = shifted(to_high, GY, 1)
     high = shifted(to_low, GY, -1)
     up, down = pl.pallas_call(
         rows_kernel,
-        out_shape=(shape(7, 32, 8, 128), shape(7, 32, 8, 128)),
-        in_specs=[vmem, vmem, vmem, pl.BlockSpec(memory_space=pl.ANY)],
+        out_shape=(shape(224, 8, 128), shape(224, 8, 128)),
+        in_specs=whole,
         out_specs=(vmem, vmem),
+        compiler_params=params,
         name="rows",
     )(e_field, h_field, material, to_low)
-    up_in = shifted(up, GX, 1)
-    down_in = shifted(down, GX, -1)
+    up_in = shifted(up, GX, 1, cyclic=False)
+    down_in = shifted(down, GX, -1, cyclic=False)
     strip, cup, cdown = pl.pallas_call(
         corner_kernel,
-        out_shape=(shape(29, 8, 128), shape(15, 8, 128), shape(15, 8, 128)),
-        in_specs=[vmem] * 3,
+        out_shape=(shape(28, 8, 128), shape(14, 8, 128), shape(14, 8, 128)),
+        in_specs=[vmem] * 2,
         out_specs=(vmem,) * 3,
+        compiler_params=params,
         name="corner",
-    )(low, high, to_low)
+    )(here(low), here(high))
     cup_in = shifted(cup, GX, 1)
     cdown_in = shifted(cdown, GX, -1)
-
-    field = pl.BlockSpec((3, 8, 8, 128), lambda i: (0, 7, 0, 0))
-    rows = pl.BlockSpec((7, 8, 8, 128), lambda i: (0, 3, 0, 0))
-    near, info = pl.pallas_call(
-        near_kernel,
-        grid=(1,),
-        out_shape=(shape(16, 2, 8, 8, 128, dtype=BF16), shape(8, 128)),
-        in_specs=[
-            field, field, pl.BlockSpec((8, 8, 128), lambda i: (7, 0, 0)), rows, rows,
-            pl.BlockSpec((29, 8, 128), lambda i: (0, 0, 0)),
-            pl.BlockSpec((15, 8, 128), lambda i: (0, 0, 0)),
-            pl.BlockSpec((15, 8, 128), lambda i: (0, 0, 0)), smem, smem,
-        ],
-        out_specs=(
-            pl.BlockSpec((16, 2, 8, 8, 128), lambda i: (0, 0, 0, 0, 0)),
-            pl.BlockSpec((8, 128), lambda i: (0, 0)),
-        ),
-        name="near",
-    )(e_field, h_field, material, up_in, down_in, strip, cup_in, cdown_in, permittivity, conductivity)
-    recv = lax.all_to_all(near.reshape(256, 8, 128), ALL, 0, 0, tiled=True)
 
     e_final, h_final = pl.pallas_call(
         yee_kernel,
@@ -454,13 +549,17 @@
             pltpu.VMEM((3, NZ, 16, 256), F32),
         ],
         cost_estimate=pl.CostEstimate(flops=40000000, transcendentals=0, bytes_accessed=8000000),
+        compiler_params=params,
         name="yee",
-    )(e_field, h_field, material, up_in, down_in, strip, cup_in, cdown_in, permittivity, conductivity)
+    )(
+        e_field, h_field, material, here(up_in), here(down_in), here(strip), here(cup_in),
+        here(cdown_in), permittivity, conductivity,
+    )
 
     partial = pl.pallas_call(
         image_kernel,
         out_shape=shape(2 * GRID, 128),
-        in_specs=[smem, smem] + [vmem] * 9,
+        in_specs=[smem, smem] + [vmem] * 9 + [pl.BlockSpec(memory_space=pl.ANY)],
         out_specs=vmem,
         scratch_shapes=[
             pltpu.VMEM((2 * K, 512), BF16),
@@ -469,10 +568,11 @@
             pltpu.VMEM((4, 256, 1024), BF16),
             pltpu.VMEM((GRID, 128), F32),
         ],
+        compiler_params=params,
         name="image",
     )(
-        info.astype(jnp.int32), info, recv.reshape(32, 8, 8, 128), tyh, tyl, txh, txl, second,
-        first, upsample, pupil_mask,
+        info.astype(jnp.int32), info, here(recv.reshape(32, 8, 8, 128)), far(tyh), far(tyl),
+        far(txh), far(txl), far(second), far(first), far(upsample), far(pupil_mask), cup,
     )
     pieces = lax.all_to_all(partial.reshape(256, 2, 128), ALL, 0, 0, tiled=True)
     image = pl.pallas_call(
@@ -480,8 +580,9 @@
         out_shape=shape(2, IMG),
         in_specs=[vmem, vmem],
         out_specs=vmem,
+        compiler_params=params,
         name="total",
-    )(pieces.reshape(512, 128), upsample)
+    )(here(pieces.reshape(512, 128)), far(upsample))
     return image, e_final, h_final
 
 

time: 118 us -> 106 us (0.90)
  the two profiles are of different devices: /device:TPU:1 before, /device:TPU:2 now
where the time goes in v2:
time: 106 us
  starting transfers between devices  52.4 us (49%)
  Pallas kernels  29.7 us (28%)
  waiting for transfers between devices  22.1 us (21%)
    ppermute x8, starting transfers between devices, shifted(): return lax.ppermute(value, axes, pairs)  22.1 us
    all_to_all x1, starting transfers between devices, local(): pieces = lax.all_to_all(partial.reshape(256, 2, 128), ALL, 0, 0, tiled=True)  16 us
    ppermute x8, waiting for transfers between devices, shifted(): return lax.ppermute(value, axes, pairs)  13.9 us
    all_to_all x1, starting transfers between devices, local(): recv = lax.all_to_all(near.reshape(256, 8, 128), ALL, 0, 0, tiled=True)  13.7 us
    pallas_call x1, Pallas kernels, local(): pl.pallas_call(yee_kernel, out_shape=(shape(*e_field.shape), shape(*h_fie...  12.1 us
    pallas_call x1, Pallas kernels, local(): pl.pallas_call(image_kernel, out_shape=shape(2 * GRID, 128), in_specs=[sm...  9.8 us
    all_to_all x1, waiting for transfers between devices, local(): recv = lax.all_to_all(near.reshape(256, 8, 128), ALL, 0, 0, tiled=True)  8.14 us
    pallas_call x1, Pallas kernels, local(): pl.pallas_call(sum_kernel, out_shape=shape(2, IMG), in_specs=[vmem, vmem]...  2.22 us
  transfers between devices with their start and end apart: 11, of which 6 were waited for; matrix products, arithmetic and copies ran while one was open for 0% of the time, Pallas kernels for 23%

profile of v2, /device:TPU:2, one launch (start us, length us, event | category | flops | bytes accessed | tf_op | source)
XLA Modules:
  0.0 105.7 jit_solution(4053395178267043857)
XLA Ops:
  0.7 0.6 copy-done.6
  1.3 1.1 %thin.1 = (f32[36,8,128]{2,1,0:T(8,128)S(1)}, f32[4,8,128]{2,1,0:T(8,128)S(1)}) custom-call(f32[3,64,8,128]{3,2,1,0:T(8,128)} %e_ref.7, f32[3,64,8,128]{3,2,1,0:T(8,128)} %h_ref.7, s32[64,8,128]{2,1,0:T(8,128)} %mat_ref.7, s32[2,8]{1,0:T(2,128)S(1)} %bitcast.7, f32[8]{0:T(128)S(1)} %copy-done.6), custom_call_target="tpu_custom_call" | custom-call | tf_op jit(solution)/shard_map/thin/pallas_call | solution.py:485
  2.5 6.6 %collective-permute-start = (f32[36,8,128]{2,1,0:T(8,128)S(1)}, f32[36,8,128]{2,1,0:T(8,128)S(1)}, u32[]{:S(2)}, u32[]{:S(2)}) collective-permute-start(f32[36,8,128]{2,1,0:T(8,128)S(1)} %get-tuple-element.16.own_ref), channel_id=1, source_target_pairs={{0,248},{8,0},{16,8},{24,16},{32,24},{40,32},{48,40},{56,48},{64,5... | collective-permute-start | bytes 442376 | tf_op jit(solution)/shard_map/ppermute | solution.py:448
  9.1 0.6 collective-permute-start.2
  9.7 4.0 %collective-permute-start.1 = (f32[4,8,128]{2,1,0:T(8,128)S(1)}, f32[4,8,128]{2,1,0:T(8,128)S(1)}, u32[]{:S(2)}, u32[]{:S(2)}) collective-permute-start(f32[4,8,128]{2,1,0:T(8,128)S(1)} %get-tuple-element.17.after_ref), channel_id=1, source_target_pairs={{0,7},{1,0},{2,1},{3,2},{4,3},{5,4},{6,5},{7,6},{8,15},{9,8},{10,9... | collective-permute-start | bytes 49160 | tf_op jit(solution)/shard_map/ppermute | solution.py:448
  13.7 1.4 %collective-permute-done.1.high_ref = f32[4,8,128]{2,1,0:T(8,128)S(1)} collective-permute-done((f32[4,8,128]{2,1,0:T(8,128)S(1)}, f32[4,8,128]{2,1,0:T(8,128)S(1)}, u32[]{:S(2)}, u32[]{:S(2)}) %collective-permute-start.1) | collective-permute-done | bytes 16416 | tf_op jit(solution)/shard_map/ppermute | solution.py:448
  15.2 2.1 %near.1 = (bf16[16,2,8,8,128]{4,3,2,1,0:T(8,128)(2,1)}, f32[8,128]{1,0:T(8,128)S(1)}) custom-call(f32[36,8,128]{2,1,0:T(8,128)S(1)} %get-tuple-element.16.own_ref, f32[36,8,128]{2,1,0:T(8,128)S(1)} %collective-permute-done.down_ref, f32[4,8,128]{2,1,0:T(8,128)S(1)} %collective-permute-done.1.high_ref, f32[4,8,128]{2,1,0:T(8,128)S(1)} %collective-permute-done.2.corner_ref, ...), custom_call_target="tpu_custom_call" | custom-call | tf_op jit(solution)/shard_map/near/pallas_call | solution.py:497
  17.3 13.7 %all-to-all-start = ((bf16[256,8,128]{2,1,0:T(8,128)(2,1)}), bf16[256,8,128]{2,1,0:T(8,128)(2,1)S(1)}, u32[]{:S(2)}, u32[]{:S(2)}) async-start(bf16[256,8,128]{2,1,0:T(8,128)(2,1)} %bitcast.1), calls=%async_computation | async-start | bytes 1048576 | tf_op jit(solution)/shard_map/all_to_all | solution.py:507
  31.1 0.9 strip.1
  31.9 1.4 %rows.1 = (f32[224,8,128]{2,1,0:T(8,128)}, f32[224,8,128]{2,1,0:T(8,128)}) custom-call(f32[3,64,8,128]{3,2,1,0:T(8,128)S(1)} %copy-done, f32[3,64,8,128]{3,2,1,0:T(8,128)S(1)} %copy-done.1, s32[64,8,128]{2,1,0:T(8,128)S(1)} %copy-done.2, f32[14,8,128]{2,1,0:T(8,128)S(1)} %get-tuple-element.21.after_ref), custom_call_target="tpu_custom_call" | custom-call | tf_op jit(solution)/shard_map/rows/pallas_call | solution.py:520
  33.3 2.1 %collective-permute-start.5 = (f32[224,8,128]{2,1,0:T(8,128)}, f32[224,8,128]{2,1,0:T(8,128)S(1)}, u32[]{:S(2)}, u32[]{:S(2)}) collective-permute-start(f32[224,8,128]{2,1,0:T(8,128)} %get-tuple-element.23), channel_id=1, source_target_pairs={{0,8},{8,16},{16,24},{24,32},{32,40},{40,48},{48,56},{56,64},{64,7... | collective-permute-start | bytes 2752520 | tf_op jit(solution)/shard_map/ppermute | solution.py:448
  35.4 1.3 %collective-permute-start.6 = (f32[224,8,128]{2,1,0:T(8,128)}, f32[224,8,128]{2,1,0:T(8,128)}, u32[]{:S(2)}, u32[]{:S(2)}) collective-permute-start(f32[224,8,128]{2,1,0:T(8,128)} %get-tuple-element.24), channel_id=1, source_target_pairs={{8,0},{16,8},{24,16},{32,24},{40,32},{48,40},{56,48},{64,56},{72,6... | collective-permute-start | bytes 2752520 | tf_op jit(solution)/shard_map/ppermute | solution.py:448
  36.7 1.5 %collective-permute-start.3 = (f32[14,8,128]{2,1,0:T(8,128)S(1)}, f32[14,8,128]{2,1,0:T(8,128)S(1)}, u32[]{:S(2)}, u32[]{:S(2)}) collective-permute-start(f32[14,8,128]{2,1,0:T(8,128)S(1)} %get-tuple-element.20), channel_id=1, source_target_pairs={{0,1},{1,2},{2,3},{3,4},{4,5},{5,6},{6,7},{7,0},{8,9},{9,10},{10,1... | collective-permute-start | bytes 172040 | tf_op jit(solution)/shard_map/ppermute | solution.py:448
  38.3 0.6 collective-permute-start.4
  38.8 2.5 %collective-permute-done.3.low_ref = f32[14,8,128]{2,1,0:T(8,128)S(1)} collective-permute-done((f32[14,8,128]{2,1,0:T(8,128)S(1)}, f32[14,8,128]{2,1,0:T(8,128)S(1)}, u32[]{:S(2)}, u32[]{:S(2)}) %collective-permute-start.3) | collective-permute-done | bytes 57376 | tf_op jit(solution)/shard_map/ppermute | solution.py:448
  41.3 2.1 %collective-permute-done.4.high_ref = f32[14,8,128]{2,1,0:T(8,128)S(1)} collective-permute-done((f32[14,8,128]{2,1,0:T(8,128)S(1)}, f32[14,8,128]{2,1,0:T(8,128)S(1)}, u32[]{:S(2)}, u32[]{:S(2)}) %collective-permute-start.4) | collective-permute-done | bytes 57376 | tf_op jit(solution)/shard_map/ppermute | solution.py:448
  43.6 8.1 %all-to-all-done = bf16[256,8,128]{2,1,0:T(8,128)(2,1)S(1)} async-done(((bf16[256,8,128]{2,1,0:T(8,128)(2,1)}), bf16[256,8,128]{2,1,0:T(8,128)(2,1)S(1)}, u32[]{:S(2)}, u32[]{:S(2)}) %all-to-all-start) | async-done | bytes 524320 | tf_op jit(solution)/shard_map/all_to_all | solution.py:507
  51.7 9.8 %image.1 = f32[512,128]{1,0:T(8,128)} custom-call(s32[8,128]{1,0:T(8,128)S(1)} %convert_element_type.3.place_ref, f32[8,128]{1,0:T(8,128)S(1)} %get-tuple-element.18.info_ref, bf16[32,8,8,128]{3,2,1,0:T(8,128)(2,1)S(1)} %bitcast.5, bf16[512,512]{1,0:T(8,128)(2,1)} %constant.14.clone.tyh_ref, bf16[512,512]{1,0:T(8,128)(2,1)} %constant.15.clone.tyl_ref, ...), custom_call_target="tpu_custom_call" | custom-call | tf_op jit(solution)/shard_map/image/pallas_call | solution.py:559
  61.5 16.0 %all-to-all-start.1 = ((f32[256,2,128]{2,1,0:T(2,128)}), f32[256,2,128]{2,1,0:T(2,128)S(1)}, u32[]{:S(2)}, u32[]{:S(2)}) async-start(f32[256,2,128]{2,1,0:T(2,128)} %bitcast.3), calls=%async_computation.1 | async-start | bytes 524288 | tf_op jit(solution)/shard_map/all_to_all | solution.py:577
  77.5 6.1 %collective-permute-start.8 = (f32[14,8,128]{2,1,0:T(8,128)S(1)}, f32[14,8,128]{2,1,0:T(8,128)S(1)}, u32[]{:S(2)}, u32[]{:S(2)}) collective-permute-start(f32[14,8,128]{2,1,0:T(8,128)S(1)} %get-tuple-element.26), channel_id=1, source_target_pairs={{0,248},{8,0},{16,8},{24,16},{32,24},{40,32},{48,40},{56,48},{64,5... | collective-permute-start | bytes 172040 | tf_op jit(solution)/shard_map/ppermute | solution.py:448
  83.6 2.2 %collective-permute-done.8.cdown_ref = f32[14,8,128]{2,1,0:T(8,128)S(1)} collective-permute-done((f32[14,8,128]{2,1,0:T(8,128)S(1)}, f32[14,8,128]{2,1,0:T(8,128)S(1)}, u32[]{:S(2)}, u32[]{:S(2)}) %collective-permute-start.8) | collective-permute-done | bytes 57376 | tf_op jit(solution)/shard_map/ppermute | solution.py:448
  85.8 5.7 %collective-permute-done.7.cup_ref = f32[14,8,128]{2,1,0:T(8,128)S(1)} collective-permute-done((f32[14,8,128]{2,1,0:T(8,128)S(1)}, f32[14,8,128]{2,1,0:T(8,128)S(1)}, u32[]{:S(2)}, u32[]{:S(2)}) %collective-permute-start.7) | collective-permute-done | bytes 57376 | tf_op jit(solution)/shard_map/ppermute | solution.py:448
  91.4 12.1 %yee.1 = (f32[3,64,8,128]{3,2,1,0:T(8,128)}, f32[3,64,8,128]{3,2,1,0:T(8,128)}) custom-call(f32[3,64,8,128]{3,2,1,0:T(8,128)S(1)} %copy-done, f32[3,64,8,128]{3,2,1,0:T(8,128)S(1)} %copy-done.1, s32[64,8,128]{2,1,0:T(8,128)S(1)} %copy-done.2, f32[224,8,128]{2,1,0:T(8,128)S(1)} %collective-permute-done.5.up_ref, ...), custom_call_target="tpu_custom_call" | custom-call | flops 40000000 | bytes 8000000 | tf_op jit(solution)/shard_map/yee/pallas_call | solution.py:541
  103.5 2.2 %total.1 = f32[2,512]{1,0:T(2,128)} custom-call(f32[512,128]{1,0:T(8,128)S(1)} %bitcast.6, f32[512,256]{1,0:T(8,128)} %constant.20.clone.up_ref), custom_call_target="tpu_custom_call" | custom-call | tf_op jit(solution)/shard_map/total/pallas_call | solution.py:578
  (21 shorter events, 0.2 us)
Async XLA Ops:
  0.6 0.7 copy-start.6
  0.6 0.7 copy-start.5
  1.3 13.8 %copy-start.3 = (f32[8]{0:T(128)S(1)}, f32[8]{0:T(128)}, u32[]{:S(2)}) copy-start(f32[8]{0:T(128)} %eps_ref.3) | copy-start | bytes 100
  1.3 13.8 %copy-start.4 = (f32[8]{0:T(128)S(1)}, f32[8]{0:T(128)}, u32[]{:S(2)}) copy-start(f32[8]{0:T(128)} %sig_ref.3) | copy-start | bytes 100
  1.3 29.7 %copy-start.1 = (f32[3,64,8,128]{3,2,1,0:T(8,128)S(1)}, f32[3,64,8,128]{3,2,1,0:T(8,128)}, u32[]{:S(2)}) copy-start(f32[3,64,8,128]{3,2,1,0:T(8,128)} %h_ref.7) | copy-start | bytes 2359300
  2.5 28.6 %copy-start = (f32[3,64,8,128]{3,2,1,0:T(8,128)S(1)}, f32[3,64,8,128]{3,2,1,0:T(8,128)}, u32[]{:S(2)}) copy-start(f32[3,64,8,128]{3,2,1,0:T(8,128)} %e_ref.7) | copy-start | bytes 2359300
  2.5 12.7 %collective-permute-start = (f32[36,8,128]{2,1,0:T(8,128)S(1)}, f32[36,8,128]{2,1,0:T(8,128)S(1)}, u32[]{:S(2)}, u32[]{:S(2)}) collective-permute-start(f32[36,8,128]{2,1,0:T(8,128)S(1)} %get-tuple-element.16.own_ref), channel_id=1, source_target_pairs={{0,248},{8,0},{16,8},{24,16},{32,24},{40,32},{48,40},{56,48},{64,5... | collective-permute-start | bytes 442376 | tf_op jit(solution)/shard_map/ppermute | solution.py:448
  9.1 4.6 %collective-permute-start.2 = (f32[4,8,128]{2,1,0:T(8,128)S(1)}, f32[4,8,128]{2,1,0:T(8,128)S(1)}, u32[]{:S(2)}, u32[]{:S(2)}) collective-permute-start(f32[4,8,128]{2,1,0:T(8,128)S(1)} %get-tuple-element.17.after_ref), channel_id=1, source_target_pairs={{0,255},{1,248},{2,249},{3,250},{4,251},{5,252},{6,253},{7,254},{8... | collective-permute-start | bytes 49160 | tf_op jit(solution)/shard_map/ppermute | solution.py:458
  9.7 5.4 %collective-permute-start.1 = (f32[4,8,128]{2,1,0:T(8,128)S(1)}, f32[4,8,128]{2,1,0:T(8,128)S(1)}, u32[]{:S(2)}, u32[]{:S(2)}) collective-permute-start(f32[4,8,128]{2,1,0:T(8,128)S(1)} %get-tuple-element.17.after_ref), channel_id=1, source_target_pairs={{0,7},{1,0},{2,1},{3,2},{4,3},{5,4},{6,5},{7,6},{8,15},{9,8},{10,9... | collective-permute-start | bytes 49160 | tf_op jit(solution)/shard_map/ppermute | solution.py:448
  17.3 13.7 %copy-start.2 = (s32[64,8,128]{2,1,0:T(8,128)S(1)}, s32[64,8,128]{2,1,0:T(8,128)}, u32[]{:S(2)}) copy-start(s32[64,8,128]{2,1,0:T(8,128)} %mat_ref.7) | copy-start | bytes 786436
  17.3 34.4 %all-to-all-start = ((bf16[256,8,128]{2,1,0:T(8,128)(2,1)}), bf16[256,8,128]{2,1,0:T(8,128)(2,1)S(1)}, u32[]{:S(2)}, u32[]{:S(2)}) async-start(bf16[256,8,128]{2,1,0:T(8,128)(2,1)} %bitcast.1), calls=%async_computation | async-start | bytes 1048576 | tf_op jit(solution)/shard_map/all_to_all | solution.py:507
  33.3 58.1 %collective-permute-start.5 = (f32[224,8,128]{2,1,0:T(8,128)}, f32[224,8,128]{2,1,0:T(8,128)S(1)}, u32[]{:S(2)}, u32[]{:S(2)}) collective-permute-start(f32[224,8,128]{2,1,0:T(8,128)} %get-tuple-element.23), channel_id=1, source_target_pairs={{0,8},{8,16},{16,24},{24,32},{32,40},{40,48},{48,56},{56,64},{64,7... | collective-permute-start | bytes 2752520 | tf_op jit(solution)/shard_map/ppermute | solution.py:448
  35.4 56.0 %collective-permute-start.6 = (f32[224,8,128]{2,1,0:T(8,128)}, f32[224,8,128]{2,1,0:T(8,128)}, u32[]{:S(2)}, u32[]{:S(2)}) collective-permute-start(f32[224,8,128]{2,1,0:T(8,128)} %get-tuple-element.24), channel_id=1, source_target_pairs={{8,0},{16,8},{24,16},{32,24},{40,32},{48,40},{56,48},{64,56},{72,6... | collective-permute-start | bytes 2752520 | tf_op jit(solution)/shard_map/ppermute | solution.py:448
  36.7 4.6 %collective-permute-start.3 = (f32[14,8,128]{2,1,0:T(8,128)S(1)}, f32[14,8,128]{2,1,0:T(8,128)S(1)}, u32[]{:S(2)}, u32[]{:S(2)}) collective-permute-start(f32[14,8,128]{2,1,0:T(8,128)S(1)} %get-tuple-element.20), channel_id=1, source_target_pairs={{0,1},{1,2},{2,3},{3,4},{4,5},{5,6},{6,7},{7,0},{8,9},{9,10},{10,1... | collective-permute-start | bytes 172040 | tf_op jit(solution)/shard_map/ppermute | solution.py:448
  38.3 5.2 %collective-permute-start.4 = (f32[14,8,128]{2,1,0:T(8,128)S(1)}, f32[14,8,128]{2,1,0:T(8,128)S(1)}, u32[]{:S(2)}, u32[]{:S(2)}) collective-permute-start(f32[14,8,128]{2,1,0:T(8,128)S(1)} %get-tuple-element.21.after_ref), channel_id=1, source_target_pairs={{0,7},{1,0},{2,1},{3,2},{4,3},{5,4},{6,5},{7,6},{8,15},{9,8},{10,9... | collective-permute-start | bytes 172040 | tf_op jit(solution)/shard_map/ppermute | solution.py:448
  61.5 42.0 %all-to-all-start.1 = ((f32[256,2,128]{2,1,0:T(2,128)}), f32[256,2,128]{2,1,0:T(2,128)S(1)}, u32[]{:S(2)}, u32[]{:S(2)}) async-start(f32[256,2,128]{2,1,0:T(2,128)} %bitcast.3), calls=%async_computation.1 | async-start | bytes 524288 | tf_op jit(solution)/shard_map/all_to_all | solution.py:577
  77.5 8.2 %collective-permute-start.8 = (f32[14,8,128]{2,1,0:T(8,128)S(1)}, f32[14,8,128]{2,1,0:T(8,128)S(1)}, u32[]{:S(2)}, u32[]{:S(2)}) collective-permute-start(f32[14,8,128]{2,1,0:T(8,128)S(1)} %get-tuple-element.26), channel_id=1, source_target_pairs={{0,248},{8,0},{16,8},{24,16},{32,24},{40,32},{48,40},{56,48},{64,5... | collective-permute-start | bytes 172040 | tf_op jit(solution)/shard_map/ppermute | solution.py:448
  83.6 7.8 %collective-permute-start.7 = (f32[14,8,128]{2,1,0:T(8,128)S(1)}, f32[14,8,128]{2,1,0:T(8,128)S(1)}, u32[]{:S(2)}, u32[]{:S(2)}) collective-permute-start(f32[14,8,128]{2,1,0:T(8,128)S(1)} %get-tuple-element.22.after_ref), channel_id=1, source_target_pairs={{0,8},{8,16},{16,24},{24,32},{32,40},{40,48},{48,56},{56,64},{64,7... | collective-permute-start | bytes 172040 | tf_op jit(solution)/shard_map/ppermute | solution.py:448

commit v3 on v2

--- a/solution.py
+++ b/solution.py
@@ -1,3 +1,5 @@
+import math
+
 import numpy as np
 import jax
 import jax.numpy as jnp
@@ -33,10 +35,19 @@
     return high, low
 
 
+def cosine_basis():
+    orders, places = np.arange(128)[:, None], np.arange(128)[None, :]
+    basis = np.cos(np.pi * orders * (2 * places + 1) / 256) * math.sqrt(2.0 / 128)
+    basis[0] *= math.sqrt(0.5)
+    return basis
+
+
 def tables(rows_all, cols_all):
     freqs = np.arange(K) - K // 2
     phase_y = 2.0 * np.pi * (np.outer(np.arange(cols_all // 2) + STEPS, freqs) % cols_all) / cols_all
     ty = np.concatenate((np.cos(phase_y), -np.sin(phase_y)), axis=1)
+    code = cosine_basis()
+    ty = np.concatenate([code @ ty[k : k + 128] for k in range(0, ty.shape[0], 128)])
     phase_x = 2.0 * np.pi * (np.outer(freqs, np.arange(rows_all) + STEPS) % rows_all) / rows_all
     tx = np.concatenate((np.cos(phase_x), np.sin(phase_x)), axis=0)
     offsets = np.arange(PW) - PW // 2
@@ -228,7 +239,7 @@
 
 
 def near_kernel(
-    own_ref, down_ref, high_ref, corner_ref, eps_ref, sig_ref, near_ref, info_ref
+    own_ref, down_ref, high_ref, corner_ref, code_ref, eps_ref, sig_ref, near_ref, info_ref
 ):
     fields = []
     for comp in range(7):
@@ -279,9 +290,16 @@
                 keep * e[z][1] + drive * (hx - h[z - 1][0] - (hz - back(hz, 0))),
                 keep * e[z][2] + drive * (hy - back(hy, 0) - (hx - back(hx, 1))),
             )
+    tiles = []
     for pol in range(2):
         tile = pltpu.roll(pltpu.roll(e[TOP - 1][pol], 12, axis=0), 252, axis=1)
-        near_ref[:, pol] = jnp.broadcast_to(tile[:8, :128].astype(BF16), (16, 8, 8, 128))
+        tiles.append(tile[:8, :128])
+    coded = jnp.dot(
+        jnp.concatenate(tiles, axis=0), code_ref[...], precision=lax.Precision.HIGHEST,
+        preferred_element_type=F32,
+    ).astype(BF16)
+    for pol in range(2):
+        near_ref[:, pol] = jnp.broadcast_to(coded[8 * pol : 8 * pol + 8], (16, 8, 8, 128))
     lane = lane_iota((8, 128))
     info = own_ref[THIN - 1]
     for k, other in enumerate((high_ref[3], down_ref[THIN - 1], corner_ref[3])):
@@ -334,32 +352,51 @@
 
     lax.fori_loop(0, NZ // 4, coef, 0)
 
+    def advance_h(z):
+        e = tuple(e_s[c, z] for c in range(3))
+        e_next = (e_s[0, z + 1], e_s[1, z + 1])
+        h = tuple(h_s[c, z + 1] for c in range(3))
+        h = magnetic(e, e_next, h, c_s[2, z])
+        for c in range(3):
+            h_s[c, z + 1] = h[c]
+        return h
+
+    def advance_e(z):
+        e = tuple(e_s[c, z] for c in range(3))
+        h = tuple(h_s[c, z + 1] for c in range(3))
+        return electric(e, h, (h_s[0, z], h_s[1, z]), c_s[0, z], c_s[1, z])
+
     def step(k, carry):
         def block(i, carry):
             first = i * BLOCK
             for j in range(BLOCK):
-                z = first + j
-                e = tuple(e_s[c, z] for c in range(3))
-                e_next = (e_s[0, z + 1], e_s[1, z + 1])
-                h = tuple(h_s[c, z + 1] for c in range(3))
-                h = magnetic(e, e_next, h, c_s[2, z])
-                for c in range(3):
-                    h_s[c, z + 1] = h[c]
+                advance_h(first + j)
             for j in range(BLOCK):
                 z = first + j
-                e = tuple(e_s[c, z] for c in range(3))
-                h = tuple(h_s[c, z + 1] for c in range(3))
-                e = electric(e, h, (h_s[0, z], h_s[1, z]), c_s[0, z], c_s[1, z])
+                e = advance_e(z)
                 for c in range(3):
                     e_s[c, z] = e[c]
             return carry
 
         return lax.fori_loop(0, NZ // BLOCK, block, carry)
 
-    lax.fori_loop(0, STEPS, step, 0)
-    for comp in range(3):
-        e_out[comp] = e_s[comp, pl.ds(0, NZ), pl.ds(0, 8), pl.ds(0, 128)]
-        h_out[comp] = h_s[comp, pl.ds(1, NZ), pl.ds(0, 8), pl.ds(0, 128)]
+    lax.fori_loop(0, STEPS - 1, step, 0)
+
+    def final(i, carry):
+        first = i * BLOCK
+        for j in range(BLOCK):
+            z = first + j
+            h = advance_h(z)
+            for c in range(3):
+                h_out[c, z] = h[c][:8, :128]
+        for j in range(BLOCK):
+            z = first + j
+            e = advance_e(z)
+            for c in range(3):
+                e_out[c, z] = e[c][:8, :128]
+        return carry
+
+    lax.fori_loop(0, NZ // BLOCK, final, 0)
 
 
 def dot(a, b):
@@ -376,7 +413,7 @@
 
 def image_kernel(
     place_ref, info_ref, recv_ref, tyh_ref, tyl_ref, txh_ref, txl_ref, second_ref, first_ref,
-    up_ref, mask_ref, after_ref, out_ref, near_s, re_s, im_s, half_s, acc_s,
+    up_ref, mask_ref, out_ref, near_s, re_s, im_s, win_s, half_s, acc_s,
 ):
     for j in range(8):
         tile = recv_ref[:, j].astype(F32).reshape(K, 128)
@@ -405,9 +442,12 @@
             window = jnp.concatenate(
                 (cut(re_s, a, b) * mask, cut(im_s, a, b) * mask), axis=1
             ).astype(BF16)
-            half = dot(window, second_ref[side]).astype(BF16)
-            half_s[i, pl.ds(0, 128), pl.ds(128 * t, 128)] = half[:, :128]
-            half_s[i, pl.ds(128, 128), pl.ds(128 * t, 128)] = half[:, 128:]
+            win_s[pl.ds(PW * t, PW)] = window
+        half = dot(win_s[...], second_ref[side]).astype(BF16)
+        for t in range(8):
+            rows = half[PW * t : PW * t + PW]
+            half_s[i, pl.ds(0, 128), pl.ds(128 * t, 128)] = rows[:, :128]
+            half_s[i, pl.ds(128, 128), pl.ds(128 * t, 128)] = rows[:, 128:]
         return carry
 
     lax.fori_loop(0, 4, cuts, 0)
@@ -497,12 +537,13 @@
     near, info = pl.pallas_call(
         near_kernel,
         out_shape=(shape(16, 2, 8, 8, 128, dtype=BF16), shape(8, 128)),
-        in_specs=[vmem] * 4 + [smem, smem],
+        in_specs=[vmem] * 5 + [smem, smem],
         out_specs=(vmem, vmem),
         compiler_params=params,
         name="near",
     )(
-        here(thin_x), here(next_x), here(next_y), here(next_xy), permittivity, conductivity
+        here(thin_x), here(next_x), here(next_y), here(next_xy),
+        here(jnp.asarray(cosine_basis().T.astype(np.float32))), permittivity, conductivity,
     )
     recv = lax.all_to_all(near.reshape(256, 8, 128), ALL, 0, 0, tiled=True)
 
@@ -559,12 +600,13 @@
     partial = pl.pallas_call(
         image_kernel,
         out_shape=shape(2 * GRID, 128),
-        in_specs=[smem, smem] + [vmem] * 9 + [pl.BlockSpec(memory_space=pl.ANY)],
+        in_specs=[smem, smem] + [vmem] * 9,
         out_specs=vmem,
         scratch_shapes=[
             pltpu.VMEM((2 * K, 512), BF16),
             pltpu.VMEM((2, K, 128), F32),
             pltpu.VMEM((2, K, 128), F32),
+            pltpu.VMEM((8 * PW, 256), BF16),
             pltpu.VMEM((4, 256, 1024), BF16),
             pltpu.VMEM((GRID, 128), F32),
         ],
@@ -572,7 +614,7 @@
         name="image",
     )(
         info.astype(jnp.int32), info, here(recv.reshape(32, 8, 8, 128)), far(tyh), far(tyl),
-        far(txh), far(txl), far(second), far(first), far(upsample), far(pupil_mask), cup,
+        far(txh), far(txl), far(second), far(first), far(upsample), far(pupil_mask),
     )
     pieces = lax.all_to_all(partial.reshape(256, 2, 128), ALL, 0, 0, tiled=True)
     image = pl.pallas_call(
@@ -582,7 +624,7 @@
         out_specs=vmem,
         compiler_params=params,
         name="total",
-    )(here(pieces.reshape(512, 128)), far(upsample))
+    )(here(pieces.reshape(512, 128)), here(upsample))
     return image, e_final, h_final
 
 

time: 106 us -> 106 us (level)
  the two profiles are of different devices: /device:TPU:2 before, /device:TPU:6 now
where the time goes in v3:
time: 106 us; the launch traced here: 105 us
  starting transfers between devices  40.5 us (38%)
  waiting for transfers between devices  35.2 us (33%)
  Pallas kernels  28.1 us (27%)
    ppermute x8, starting transfers between devices, shifted(): return lax.ppermute(value, axes, pairs)  22.7 us
    ppermute x8, waiting for transfers between devices, shifted(): return lax.ppermute(value, axes, pairs)  13.9 us
    all_to_all x1, waiting for transfers between devices, local(): recv = lax.all_to_all(near.reshape(256, 8, 128), ALL, 0, 0, tiled=True)  13.6 us
    pallas_call x1, Pallas kernels, local(): pl.pallas_call(yee_kernel, out_shape=(shape(*e_field.shape), shape(*h_fie...  11.4 us
    pallas_call x1, Pallas kernels, local(): pl.pallas_call(image_kernel, out_shape=shape(2 * GRID, 128), in_specs=[sm...  9.73 us
    all_to_all x1, starting transfers between devices, local(): recv = lax.all_to_all(near.reshape(256, 8, 128), ALL, 0, 0, tiled=True)  8.92 us
    all_to_all x1, starting transfers between devices, local(): pieces = lax.all_to_all(partial.reshape(256, 2, 128), ALL, 0, 0, tiled=True)  8.01 us
    ppermute x1, waiting for transfers between devices, diagonal(): return lax.ppermute(value, ALL, pairs)  7.7 us
  transfers between devices with their start and end apart: 11, of which 6 were waited for; matrix products, arithmetic and copies ran while one was open for 0% of the time, Pallas kernels for 22%

profile of v3, /device:TPU:6, one launch (start us, length us, event | category | flops | bytes accessed | tf_op | source)
XLA Modules:
  0.0 105.4 jit_solution(454544977069252087)
XLA Ops:
  0.7 0.6 copy-done.10
  1.3 1.1 %thin.1 = (f32[36,8,128]{2,1,0:T(8,128)S(1)}, f32[4,8,128]{2,1,0:T(8,128)S(1)}) custom-call(f32[3,64,8,128]{3,2,1,0:T(8,128)} %e_ref.7, f32[3,64,8,128]{3,2,1,0:T(8,128)} %h_ref.7, s32[64,8,128]{2,1,0:T(8,128)} %mat_ref.7, s32[2,8]{1,0:T(2,128)S(1)} %bitcast.7, f32[8]{0:T(128)S(1)} %copy-done.10), custom_call_target="tpu_custom_call" | custom-call | tf_op jit(solution)/shard_map/thin/pallas_call | solution.py:525
  2.5 6.6 %collective-permute-start = (f32[36,8,128]{2,1,0:T(8,128)S(1)}, f32[36,8,128]{2,1,0:T(8,128)S(1)}, u32[]{:S(2)}, u32[]{:S(2)}) collective-permute-start(f32[36,8,128]{2,1,0:T(8,128)S(1)} %get-tuple-element.16.own_ref), channel_id=1, source_target_pairs={{0,248},{8,0},{16,8},{24,16},{32,24},{40,32},{48,40},{56,48},{64,5... | collective-permute-start | bytes 442376 | tf_op jit(solution)/shard_map/ppermute | solution.py:488
  9.1 0.9 collective-permute-start.2
  10.0 0.5 collective-permute-start.1
  10.6 7.7 %collective-permute-done.2.corner_ref = f32[4,8,128]{2,1,0:T(8,128)S(1)} collective-permute-done((f32[4,8,128]{2,1,0:T(8,128)S(1)}, f32[4,8,128]{2,1,0:T(8,128)S(1)}, u32[]{:S(2)}, u32[]{:S(2)}) %collective-permute-start.2) | collective-permute-done | bytes 16416 | tf_op jit(solution)/shard_map/ppermute | solution.py:498
  18.3 1.6 %collective-permute-done.1.high_ref = f32[4,8,128]{2,1,0:T(8,128)S(1)} collective-permute-done((f32[4,8,128]{2,1,0:T(8,128)S(1)}, f32[4,8,128]{2,1,0:T(8,128)S(1)}, u32[]{:S(2)}, u32[]{:S(2)}) %collective-permute-start.1) | collective-permute-done | bytes 16416 | tf_op jit(solution)/shard_map/ppermute | solution.py:488
  19.9 2.3 %near.1 = (bf16[16,2,8,8,128]{4,3,2,1,0:T(8,128)(2,1)}, f32[8,128]{1,0:T(8,128)S(1)}) custom-call(f32[36,8,128]{2,1,0:T(8,128)S(1)} %get-tuple-element.16.own_ref, f32[36,8,128]{2,1,0:T(8,128)S(1)} %collective-permute-done.down_ref, f32[4,8,128]{2,1,0:T(8,128)S(1)} %collective-permute-done.1.high_ref, f32[4,8,128]{2,1,0:T(8,128)S(1)} %collective-permute-done.2.corner_ref, ...), custom_call_target="tpu_custom_call" | custom-call | tf_op jit(solution)/shard_map/near/pallas_call | solution.py:537
  22.2 8.9 %all-to-all-start = ((bf16[256,8,128]{2,1,0:T(8,128)(2,1)}), bf16[256,8,128]{2,1,0:T(8,128)(2,1)S(1)}, u32[]{:S(2)}, u32[]{:S(2)}) async-start(bf16[256,8,128]{2,1,0:T(8,128)(2,1)} %bitcast.1), calls=%async_computation | async-start | bytes 1048576 | tf_op jit(solution)/shard_map/all_to_all | solution.py:548
  31.2 0.9 strip.1
  32.1 1.4 %rows.1 = (f32[224,8,128]{2,1,0:T(8,128)}, f32[224,8,128]{2,1,0:T(8,128)}) custom-call(f32[3,64,8,128]{3,2,1,0:T(8,128)S(1)} %copy-done, f32[3,64,8,128]{3,2,1,0:T(8,128)S(1)} %copy-done.1, s32[64,8,128]{2,1,0:T(8,128)S(1)} %copy-done.2, f32[14,8,128]{2,1,0:T(8,128)S(1)} %get-tuple-element.20.after_ref), custom_call_target="tpu_custom_call" | custom-call | tf_op jit(solution)/shard_map/rows/pallas_call | solution.py:561
  33.5 2.1 %collective-permute-start.3 = (f32[224,8,128]{2,1,0:T(8,128)}, f32[224,8,128]{2,1,0:T(8,128)S(1)}, u32[]{:S(2)}, u32[]{:S(2)}) collective-permute-start(f32[224,8,128]{2,1,0:T(8,128)} %get-tuple-element.21), channel_id=1, source_target_pairs={{0,8},{8,16},{16,24},{24,32},{32,40},{40,48},{48,56},{56,64},{64,7... | collective-permute-start | bytes 2752520 | tf_op jit(solution)/shard_map/ppermute | solution.py:488
  35.5 1.3 %collective-permute-start.4 = (f32[224,8,128]{2,1,0:T(8,128)}, f32[224,8,128]{2,1,0:T(8,128)}, u32[]{:S(2)}, u32[]{:S(2)}) collective-permute-start(f32[224,8,128]{2,1,0:T(8,128)} %get-tuple-element.22), channel_id=1, source_target_pairs={{8,0},{16,8},{24,16},{32,24},{40,32},{48,40},{56,48},{64,56},{72,6... | collective-permute-start | bytes 2752520 | tf_op jit(solution)/shard_map/ppermute | solution.py:488
  36.9 13.6 %all-to-all-done = bf16[256,8,128]{2,1,0:T(8,128)(2,1)S(1)} async-done(((bf16[256,8,128]{2,1,0:T(8,128)(2,1)}), bf16[256,8,128]{2,1,0:T(8,128)(2,1)S(1)}, u32[]{:S(2)}, u32[]{:S(2)}) %all-to-all-start) | async-done | bytes 524320 | tf_op jit(solution)/shard_map/all_to_all | solution.py:548
  50.4 9.7 %image.1 = f32[512,128]{1,0:T(8,128)} custom-call(s32[8,128]{1,0:T(8,128)S(1)} %convert_element_type.3.place_ref, f32[8,128]{1,0:T(8,128)S(1)} %get-tuple-element.18.info_ref, bf16[32,8,8,128]{3,2,1,0:T(8,128)(2,1)S(1)} %bitcast.5, bf16[512,512]{1,0:T(8,128)(2,1)} %constant.16.clone.tyh_ref, bf16[512,512]{1,0:T(8,128)(2,1)} %constant.17.clone.tyl_ref, ...), custom_call_target="tpu_custom_call" | custom-call | tf_op jit(solution)/shard_map/image/pallas_call | solution.py:600
  60.2 8.0 %all-to-all-start.1 = ((f32[256,2,128]{2,1,0:T(2,128)}), f32[256,2,128]{2,1,0:T(2,128)S(1)}, u32[]{:S(2)}, u32[]{:S(2)}) async-start(f32[256,2,128]{2,1,0:T(2,128)} %bitcast.3), calls=%async_computation.1 | async-start | bytes 524288 | tf_op jit(solution)/shard_map/all_to_all | solution.py:619
  68.2 6.5 %collective-permute-start.5 = (f32[14,8,128]{2,1,0:T(8,128)S(1)}, f32[14,8,128]{2,1,0:T(8,128)S(1)}, u32[]{:S(2)}, u32[]{:S(2)}) collective-permute-start(f32[14,8,128]{2,1,0:T(8,128)S(1)} %copy-done.12), channel_id=1, source_target_pairs={{0,1},{1,2},{2,3},{3,4},{4,5},{5,6},{6,7},{7,0},{8,9},{9,10},{10,1... | collective-permute-start | bytes 172040 | tf_op jit(solution)/shard_map/ppermute | solution.py:488
  74.7 2.5 %collective-permute-done.5.low_ref = f32[14,8,128]{2,1,0:T(8,128)S(1)} collective-permute-done((f32[14,8,128]{2,1,0:T(8,128)S(1)}, f32[14,8,128]{2,1,0:T(8,128)S(1)}, u32[]{:S(2)}, u32[]{:S(2)}) %collective-permute-start.5) | collective-permute-done | bytes 57376 | tf_op jit(solution)/shard_map/ppermute | solution.py:488
  77.1 7.9 %collective-permute-done.6.high_ref = f32[14,8,128]{2,1,0:T(8,128)S(1)} collective-permute-done((f32[14,8,128]{2,1,0:T(8,128)S(1)}, f32[14,8,128]{2,1,0:T(8,128)S(1)}, u32[]{:S(2)}, u32[]{:S(2)}) %collective-permute-start.6) | collective-permute-done | bytes 57376 | tf_op jit(solution)/shard_map/ppermute | solution.py:488
  85.1 0.1 corner.1
  85.3 5.6 %collective-permute-start.8 = (f32[14,8,128]{2,1,0:T(8,128)S(1)}, f32[14,8,128]{2,1,0:T(8,128)S(1)}, u32[]{:S(2)}, u32[]{:S(2)}) collective-permute-start(f32[14,8,128]{2,1,0:T(8,128)S(1)} %get-tuple-element.26), channel_id=1, source_target_pairs={{0,248},{8,0},{16,8},{24,16},{32,24},{40,32},{48,40},{56,48},{64,5... | collective-permute-start | bytes 172040 | tf_op jit(solution)/shard_map/ppermute | solution.py:488
  90.9 1.9 %collective-permute-done.7.cup_ref = f32[14,8,128]{2,1,0:T(8,128)S(1)} collective-permute-done((f32[14,8,128]{2,1,0:T(8,128)S(1)}, f32[14,8,128]{2,1,0:T(8,128)S(1)}, u32[]{:S(2)}, u32[]{:S(2)}) %collective-permute-start.7) | collective-permute-done | bytes 57376 | tf_op jit(solution)/shard_map/ppermute | solution.py:488
  92.8 11.4 %yee.1 = (f32[3,64,8,128]{3,2,1,0:T(8,128)}, f32[3,64,8,128]{3,2,1,0:T(8,128)}) custom-call(f32[3,64,8,128]{3,2,1,0:T(8,128)S(1)} %copy-done, f32[3,64,8,128]{3,2,1,0:T(8,128)S(1)} %copy-done.1, s32[64,8,128]{2,1,0:T(8,128)S(1)} %copy-done.2, f32[224,8,128]{2,1,0:T(8,128)S(1)} %collective-permute-done.3.up_ref, ...), custom_call_target="tpu_custom_call" | custom-call | flops 40000000 | bytes 8000000 | tf_op jit(solution)/shard_map/yee/pallas_call | solution.py:582
  104.2 1.2 %total.1 = f32[2,512]{1,0:T(2,128)} custom-call(f32[512,128]{1,0:T(8,128)S(1)} %bitcast.6, f32[512,256]{1,0:T(8,128)S(1)} %copy-done.3), custom_call_target="tpu_custom_call" | custom-call | tf_op jit(solution)/shard_map/total/pallas_call | solution.py:620
  (33 shorter events, 0.2 us)
Async XLA Ops:
  0.6 0.7 copy-start.10
  0.6 0.7 copy-start.9
  1.3 18.6 %copy-start.4 = (f32[128,128]{1,0:T(8,128)S(1)}, f32[128,128]{1,0:T(8,128)}, u32[]{:S(2)}) copy-start(f32[128,128]{1,0:T(8,128)} %constant.23.clone.code_ref) | copy-start | bytes 196612
  1.3 18.6 %copy-start.7 = (f32[8]{0:T(128)S(1)}, f32[8]{0:T(128)}, u32[]{:S(2)}) copy-start(f32[8]{0:T(128)} %eps_ref.3) | copy-start | bytes 100
  1.3 18.6 %copy-start.8 = (f32[8]{0:T(128)S(1)}, f32[8]{0:T(128)}, u32[]{:S(2)}) copy-start(f32[8]{0:T(128)} %sig_ref.3) | copy-start | bytes 100
  1.3 29.8 %copy-start.1 = (f32[3,64,8,128]{3,2,1,0:T(8,128)S(1)}, f32[3,64,8,128]{3,2,1,0:T(8,128)}, u32[]{:S(2)}) copy-start(f32[3,64,8,128]{3,2,1,0:T(8,128)} %h_ref.7) | copy-start | bytes 2359300
  2.5 28.7 %copy-start = (f32[3,64,8,128]{3,2,1,0:T(8,128)S(1)}, f32[3,64,8,128]{3,2,1,0:T(8,128)}, u32[]{:S(2)}) copy-start(f32[3,64,8,128]{3,2,1,0:T(8,128)} %e_ref.7) | copy-start | bytes 2359300
  2.5 17.4 %collective-permute-start = (f32[36,8,128]{2,1,0:T(8,128)S(1)}, f32[36,8,128]{2,1,0:T(8,128)S(1)}, u32[]{:S(2)}, u32[]{:S(2)}) collective-permute-start(f32[36,8,128]{2,1,0:T(8,128)S(1)} %get-tuple-element.16.own_ref), channel_id=1, source_target_pairs={{0,248},{8,0},{16,8},{24,16},{32,24},{40,32},{48,40},{56,48},{64,5... | collective-permute-start | bytes 442376 | tf_op jit(solution)/shard_map/ppermute | solution.py:488
  9.1 9.2 %collective-permute-start.2 = (f32[4,8,128]{2,1,0:T(8,128)S(1)}, f32[4,8,128]{2,1,0:T(8,128)S(1)}, u32[]{:S(2)}, u32[]{:S(2)}) collective-permute-start(f32[4,8,128]{2,1,0:T(8,128)S(1)} %get-tuple-element.17.after_ref), channel_id=1, source_target_pairs={{0,255},{1,248},{2,249},{3,250},{4,251},{5,252},{6,253},{7,254},{8... | collective-permute-start | bytes 49160 | tf_op jit(solution)/shard_map/ppermute | solution.py:498
  10.0 9.9 %collective-permute-start.1 = (f32[4,8,128]{2,1,0:T(8,128)S(1)}, f32[4,8,128]{2,1,0:T(8,128)S(1)}, u32[]{:S(2)}, u32[]{:S(2)}) collective-permute-start(f32[4,8,128]{2,1,0:T(8,128)S(1)} %get-tuple-element.17.after_ref), channel_id=1, source_target_pairs={{0,7},{1,0},{2,1},{3,2},{4,3},{5,4},{6,5},{7,6},{8,15},{9,8},{10,9... | collective-permute-start | bytes 49160 | tf_op jit(solution)/shard_map/ppermute | solution.py:488
  22.2 8.9 %copy-start.2 = (s32[64,8,128]{2,1,0:T(8,128)S(1)}, s32[64,8,128]{2,1,0:T(8,128)}, u32[]{:S(2)}) copy-start(s32[64,8,128]{2,1,0:T(8,128)} %mat_ref.7) | copy-start | bytes 786436
  22.2 28.2 %all-to-all-start = ((bf16[256,8,128]{2,1,0:T(8,128)(2,1)}), bf16[256,8,128]{2,1,0:T(8,128)(2,1)S(1)}, u32[]{:S(2)}, u32[]{:S(2)}) async-start(bf16[256,8,128]{2,1,0:T(8,128)(2,1)} %bitcast.1), calls=%async_computation | async-start | bytes 1048576 | tf_op jit(solution)/shard_map/all_to_all | solution.py:548
  32.0 1.4 %copy-start.5 = (f32[14,8,128]{2,1,0:T(8,128)}, f32[14,8,128]{2,1,0:T(8,128)S(1)}, u32[]{:S(2)}) copy-start(f32[14,8,128]{2,1,0:T(8,128)S(1)} %get-tuple-element.20.after_ref) | copy-start | bytes 172036
  32.0 1.4 %copy-start.11 = (f32[14,8,128]{2,1,0:T(8,128)}, f32[14,8,128]{2,1,0:T(8,128)S(1)}, u32[]{:S(2)}) copy-start(f32[14,8,128]{2,1,0:T(8,128)S(1)} %get-tuple-element.23) | copy-start | bytes 172036
  33.5 59.3 %collective-permute-start.3 = (f32[224,8,128]{2,1,0:T(8,128)}, f32[224,8,128]{2,1,0:T(8,128)S(1)}, u32[]{:S(2)}, u32[]{:S(2)}) collective-permute-start(f32[224,8,128]{2,1,0:T(8,128)} %get-tuple-element.21), channel_id=1, source_target_pairs={{0,8},{8,16},{16,24},{24,32},{32,40},{40,48},{48,56},{56,64},{64,7... | collective-permute-start | bytes 2752520 | tf_op jit(solution)/shard_map/ppermute | solution.py:488
  35.5 57.2 %collective-permute-start.4 = (f32[224,8,128]{2,1,0:T(8,128)}, f32[224,8,128]{2,1,0:T(8,128)}, u32[]{:S(2)}, u32[]{:S(2)}) collective-permute-start(f32[224,8,128]{2,1,0:T(8,128)} %get-tuple-element.22), channel_id=1, source_target_pairs={{8,0},{16,8},{24,16},{32,24},{40,32},{48,40},{56,48},{64,56},{72,6... | collective-permute-start | bytes 2752520 | tf_op jit(solution)/shard_map/ppermute | solution.py:488
  60.2 8.0 %copy-start.12 = (f32[14,8,128]{2,1,0:T(8,128)S(1)}, f32[14,8,128]{2,1,0:T(8,128)}, u32[]{:S(2)}) copy-start(f32[14,8,128]{2,1,0:T(8,128)} %copy-done.11) | copy-start | bytes 172036
  60.2 14.5 %copy-start.6 = (f32[14,8,128]{2,1,0:T(8,128)S(1)}, f32[14,8,128]{2,1,0:T(8,128)}, u32[]{:S(2)}) copy-start(f32[14,8,128]{2,1,0:T(8,128)} %copy-done.5) | copy-start | bytes 172036
  60.2 44.0 %all-to-all-start.1 = ((f32[256,2,128]{2,1,0:T(2,128)}), f32[256,2,128]{2,1,0:T(2,128)S(1)}, u32[]{:S(2)}, u32[]{:S(2)}) async-start(f32[256,2,128]{2,1,0:T(2,128)} %bitcast.3), calls=%async_computation.1 | async-start | bytes 524288 | tf_op jit(solution)/shard_map/all_to_all | solution.py:619
  68.2 9.0 %collective-permute-start.5 = (f32[14,8,128]{2,1,0:T(8,128)S(1)}, f32[14,8,128]{2,1,0:T(8,128)S(1)}, u32[]{:S(2)}, u32[]{:S(2)}) collective-permute-start(f32[14,8,128]{2,1,0:T(8,128)S(1)} %copy-done.12), channel_id=1, source_target_pairs={{0,1},{1,2},{2,3},{3,4},{4,5},{5,6},{6,7},{7,0},{8,9},{9,10},{10,1... | collective-permute-start | bytes 172040 | tf_op jit(solution)/shard_map/ppermute | solution.py:488
  74.7 10.4 %collective-permute-start.6 = (f32[14,8,128]{2,1,0:T(8,128)S(1)}, f32[14,8,128]{2,1,0:T(8,128)S(1)}, u32[]{:S(2)}, u32[]{:S(2)}) collective-permute-start(f32[14,8,128]{2,1,0:T(8,128)S(1)} %copy-done.6), channel_id=1, source_target_pairs={{0,7},{1,0},{2,1},{3,2},{4,3},{5,4},{6,5},{7,6},{8,15},{9,8},{10,9... | collective-permute-start | bytes 172040 | tf_op jit(solution)/shard_map/ppermute | solution.py:488
  85.2 7.6 %collective-permute-start.7 = (f32[14,8,128]{2,1,0:T(8,128)S(1)}, f32[14,8,128]{2,1,0:T(8,128)S(1)}, u32[]{:S(2)}, u32[]{:S(2)}) collective-permute-start(f32[14,8,128]{2,1,0:T(8,128)S(1)} %get-tuple-element.25), channel_id=1, source_target_pairs={{0,8},{8,16},{16,24},{24,32},{32,40},{40,48},{48,56},{56,64},{64,7... | collective-permute-start | bytes 172040 | tf_op jit(solution)/shard_map/ppermute | solution.py:488
  85.3 7.5 %collective-permute-start.8 = (f32[14,8,128]{2,1,0:T(8,128)S(1)}, f32[14,8,128]{2,1,0:T(8,128)S(1)}, u32[]{:S(2)}, u32[]{:S(2)}) collective-permute-start(f32[14,8,128]{2,1,0:T(8,128)S(1)} %get-tuple-element.26), channel_id=1, source_target_pairs={{0,248},{8,0},{16,8},{24,16},{32,24},{40,32},{48,40},{56,48},{64,5... | collective-permute-start | bytes 172040 | tf_op jit(solution)/shard_map/ppermute | solution.py:488
  92.8 11.4 %copy-start.3 = (f32[512,256]{1,0:T(8,128)S(1)}, f32[512,256]{1,0:T(8,128)}, u32[]{:S(2)}) copy-start(f32[512,256]{1,0:T(8,128)} %constant.22.clone.up_ref) | copy-start | bytes 1572868

commit v4 on v3

--- a/solution.py
+++ b/solution.py
@@ -404,11 +404,10 @@
 
 
 def cut(ref, a, b):
-    turn = (128 - b) % 128
-    first = pltpu.roll(ref[0, pl.ds(a, PW), :], turn, axis=1)
-    second = pltpu.roll(ref[1, pl.ds(a, PW), :], turn, axis=1)
-    lane = lane_iota((PW, 128))
-    return jnp.where(lane + b < 128, first, second)
+    merged = jnp.where(
+        lane_iota((PW, 128)) >= b, ref[0, pl.ds(a, PW), :], ref[1, pl.ds(a, PW), :]
+    )
+    return pltpu.roll(merged, (128 - b) % 128, axis=1)
 
 
 def image_kernel(
@@ -530,7 +529,7 @@
         out_specs=(thin, head),
         compiler_params=params,
         name="thin",
-    )(far(e_field), far(h_field), far(material), src_shift.T, src_weight)
+    )(far(e_field), far(h_field), far(material), far(src_shift.T), far(src_weight))
     next_xy = diagonal(thin_y)
     next_y = shifted(thin_y, GY, -1)
     next_x = shifted(thin_x, GX, -1)

time: 106 us -> 104 us (0.981)
  no operation moved by 1% of the time
where the time goes in v4:
time: 104 us
  starting transfers between devices  40.6 us (39%)
  waiting for transfers between devices  35.2 us (34%)
  Pallas kernels  27.1 us (26%)
    ppermute x8, starting transfers between devices, shifted(): return lax.ppermute(value, axes, pairs)  22.7 us
    ppermute x8, waiting for transfers between devices, shifted(): return lax.ppermute(value, axes, pairs)  13.9 us
    all_to_all x1, waiting for transfers between devices, local(): recv = lax.all_to_all(near.reshape(256, 8, 128), ALL, 0, 0, tiled=True)  13.6 us
    pallas_call x1, Pallas kernels, local(): pl.pallas_call(yee_kernel, out_shape=(shape(*e_field.shape), shape(*h_fie...  11.4 us
    all_to_all x1, starting transfers between devices, local(): recv = lax.all_to_all(near.reshape(256, 8, 128), ALL, 0, 0, tiled=True)  8.92 us
    pallas_call x1, Pallas kernels, local(): pl.pallas_call(image_kernel, out_shape=shape(2 * GRID, 128), in_specs=[sm...  8.7 us
    all_to_all x1, starting transfers between devices, local(): pieces = lax.all_to_all(partial.reshape(256, 2, 128), ALL, 0, 0, tiled=True)  8.08 us
    ppermute x1, waiting for transfers between devices, diagonal(): return lax.ppermute(value, ALL, pairs)  7.7 us
  transfers between devices with their start and end apart: 11, of which 6 were waited for; matrix products, arithmetic and copies ran while one was open for 0% of the time, Pallas kernels for 22%

profile of v4, /device:TPU:6, one launch (start us, length us, event | category | flops | bytes accessed | tf_op | source)
XLA Modules:
  0.0 103.7 jit_solution(12256949801200064663)
XLA Ops:
  0.7 1.1 %thin.1 = (f32[36,8,128]{2,1,0:T(8,128)S(1)}, f32[4,8,128]{2,1,0:T(8,128)S(1)}) custom-call(f32[3,64,8,128]{3,2,1,0:T(8,128)} %e_ref.7, f32[3,64,8,128]{3,2,1,0:T(8,128)} %h_ref.7, s32[64,8,128]{2,1,0:T(8,128)} %mat_ref.7, s32[2,8]{1,0:T(2,128)} %bitcast.7, f32[8]{0:T(128)} %weight_ref.1), custom_call_target="tpu_custom_call" | custom-call | tf_op jit(solution)/shard_map/thin/pallas_call | solution.py:524
  1.8 6.6 %collective-permute-start = (f32[36,8,128]{2,1,0:T(8,128)S(1)}, f32[36,8,128]{2,1,0:T(8,128)S(1)}, u32[]{:S(2)}, u32[]{:S(2)}) collective-permute-start(f32[36,8,128]{2,1,0:T(8,128)S(1)} %get-tuple-element.16.own_ref), channel_id=1, source_target_pairs={{0,248},{8,0},{16,8},{24,16},{32,24},{40,32},{48,40},{56,48},{64,5... | collective-permute-start | bytes 442376 | tf_op jit(solution)/shard_map/ppermute | solution.py:487
  8.4 0.9 collective-permute-start.2
  9.4 0.5 collective-permute-start.1
  9.9 7.7 %collective-permute-done.2.corner_ref = f32[4,8,128]{2,1,0:T(8,128)S(1)} collective-permute-done((f32[4,8,128]{2,1,0:T(8,128)S(1)}, f32[4,8,128]{2,1,0:T(8,128)S(1)}, u32[]{:S(2)}, u32[]{:S(2)}) %collective-permute-start.2) | collective-permute-done | bytes 16416 | tf_op jit(solution)/shard_map/ppermute | solution.py:497
  17.6 1.6 %collective-permute-done.1.high_ref = f32[4,8,128]{2,1,0:T(8,128)S(1)} collective-permute-done((f32[4,8,128]{2,1,0:T(8,128)S(1)}, f32[4,8,128]{2,1,0:T(8,128)S(1)}, u32[]{:S(2)}, u32[]{:S(2)}) %collective-permute-start.1) | collective-permute-done | bytes 16416 | tf_op jit(solution)/shard_map/ppermute | solution.py:487
  19.3 2.3 %near.1 = (bf16[16,2,8,8,128]{4,3,2,1,0:T(8,128)(2,1)}, f32[8,128]{1,0:T(8,128)S(1)}) custom-call(f32[36,8,128]{2,1,0:T(8,128)S(1)} %get-tuple-element.16.own_ref, f32[36,8,128]{2,1,0:T(8,128)S(1)} %collective-permute-done.down_ref, f32[4,8,128]{2,1,0:T(8,128)S(1)} %collective-permute-done.1.high_ref, f32[4,8,128]{2,1,0:T(8,128)S(1)} %collective-permute-done.2.corner_ref, ...), custom_call_target="tpu_custom_call" | custom-call | tf_op jit(solution)/shard_map/near/pallas_call | solution.py:536
  21.6 8.9 %all-to-all-start = ((bf16[256,8,128]{2,1,0:T(8,128)(2,1)}), bf16[256,8,128]{2,1,0:T(8,128)(2,1)S(1)}, u32[]{:S(2)}, u32[]{:S(2)}) async-start(bf16[256,8,128]{2,1,0:T(8,128)(2,1)} %bitcast.1), calls=%async_computation | async-start | bytes 1048576 | tf_op jit(solution)/shard_map/all_to_all | solution.py:547
  30.5 0.9 strip.1
  31.4 1.4 %rows.1 = (f32[224,8,128]{2,1,0:T(8,128)}, f32[224,8,128]{2,1,0:T(8,128)}) custom-call(f32[3,64,8,128]{3,2,1,0:T(8,128)S(1)} %copy-done, f32[3,64,8,128]{3,2,1,0:T(8,128)S(1)} %copy-done.1, s32[64,8,128]{2,1,0:T(8,128)S(1)} %copy-done.2, f32[14,8,128]{2,1,0:T(8,128)S(1)} %get-tuple-element.20.after_ref), custom_call_target="tpu_custom_call" | custom-call | tf_op jit(solution)/shard_map/rows/pallas_call | solution.py:560
  32.8 2.1 %collective-permute-start.3 = (f32[224,8,128]{2,1,0:T(8,128)}, f32[224,8,128]{2,1,0:T(8,128)S(1)}, u32[]{:S(2)}, u32[]{:S(2)}) collective-permute-start(f32[224,8,128]{2,1,0:T(8,128)} %get-tuple-element.21), channel_id=1, source_target_pairs={{0,8},{8,16},{16,24},{24,32},{32,40},{40,48},{48,56},{56,64},{64,7... | collective-permute-start | bytes 2752520 | tf_op jit(solution)/shard_map/ppermute | solution.py:487
  34.9 1.3 %collective-permute-start.4 = (f32[224,8,128]{2,1,0:T(8,128)}, f32[224,8,128]{2,1,0:T(8,128)}, u32[]{:S(2)}, u32[]{:S(2)}) collective-permute-start(f32[224,8,128]{2,1,0:T(8,128)} %get-tuple-element.22), channel_id=1, source_target_pairs={{8,0},{16,8},{24,16},{32,24},{40,32},{48,40},{56,48},{64,56},{72,6... | collective-permute-start | bytes 2752520 | tf_op jit(solution)/shard_map/ppermute | solution.py:487
  36.2 13.6 %all-to-all-done = bf16[256,8,128]{2,1,0:T(8,128)(2,1)S(1)} async-done(((bf16[256,8,128]{2,1,0:T(8,128)(2,1)}), bf16[256,8,128]{2,1,0:T(8,128)(2,1)S(1)}, u32[]{:S(2)}, u32[]{:S(2)}) %all-to-all-start) | async-done | bytes 524320 | tf_op jit(solution)/shard_map/all_to_all | solution.py:547
  49.8 8.7 %image.1 = f32[512,128]{1,0:T(8,128)} custom-call(s32[8,128]{1,0:T(8,128)S(1)} %convert_element_type.3.place_ref, f32[8,128]{1,0:T(8,128)S(1)} %get-tuple-element.18.info_ref, bf16[32,8,8,128]{3,2,1,0:T(8,128)(2,1)S(1)} %bitcast.5, bf16[512,512]{1,0:T(8,128)(2,1)} %constant.16.clone.tyh_ref, bf16[512,512]{1,0:T(8,128)(2,1)} %constant.17.clone.tyl_ref, ...), custom_call_target="tpu_custom_call" | custom-call | tf_op jit(solution)/shard_map/image/pallas_call | solution.py:599
  58.5 8.1 %all-to-all-start.1 = ((f32[256,2,128]{2,1,0:T(2,128)}), f32[256,2,128]{2,1,0:T(2,128)S(1)}, u32[]{:S(2)}, u32[]{:S(2)}) async-start(f32[256,2,128]{2,1,0:T(2,128)} %bitcast.3), calls=%async_computation.1 | async-start | bytes 524288 | tf_op jit(solution)/shard_map/all_to_all | solution.py:618
  66.6 6.5 %collective-permute-start.5 = (f32[14,8,128]{2,1,0:T(8,128)S(1)}, f32[14,8,128]{2,1,0:T(8,128)S(1)}, u32[]{:S(2)}, u32[]{:S(2)}) collective-permute-start(f32[14,8,128]{2,1,0:T(8,128)S(1)} %copy-done.10), channel_id=1, source_target_pairs={{0,1},{1,2},{2,3},{3,4},{4,5},{5,6},{6,7},{7,0},{8,9},{9,10},{10,1... | collective-permute-start | bytes 172040 | tf_op jit(solution)/shard_map/ppermute | solution.py:487
  73.0 2.5 %collective-permute-done.5.low_ref = f32[14,8,128]{2,1,0:T(8,128)S(1)} collective-permute-done((f32[14,8,128]{2,1,0:T(8,128)S(1)}, f32[14,8,128]{2,1,0:T(8,128)S(1)}, u32[]{:S(2)}, u32[]{:S(2)}) %collective-permute-start.5) | collective-permute-done | bytes 57376 | tf_op jit(solution)/shard_map/ppermute | solution.py:487
  75.5 7.9 %collective-permute-done.6.high_ref = f32[14,8,128]{2,1,0:T(8,128)S(1)} collective-permute-done((f32[14,8,128]{2,1,0:T(8,128)S(1)}, f32[14,8,128]{2,1,0:T(8,128)S(1)}, u32[]{:S(2)}, u32[]{:S(2)}) %collective-permute-start.6) | collective-permute-done | bytes 57376 | tf_op jit(solution)/shard_map/ppermute | solution.py:487
  83.4 0.1 corner.1
  83.5 0.1 collective-permute-start.7
  83.6 5.6 %collective-permute-start.8 = (f32[14,8,128]{2,1,0:T(8,128)S(1)}, f32[14,8,128]{2,1,0:T(8,128)S(1)}, u32[]{:S(2)}, u32[]{:S(2)}) collective-permute-start(f32[14,8,128]{2,1,0:T(8,128)S(1)} %get-tuple-element.26), channel_id=1, source_target_pairs={{0,248},{8,0},{16,8},{24,16},{32,24},{40,32},{48,40},{56,48},{64,5... | collective-permute-start | bytes 172040 | tf_op jit(solution)/shard_map/ppermute | solution.py:487
  89.3 1.9 %collective-permute-done.7.cup_ref = f32[14,8,128]{2,1,0:T(8,128)S(1)} collective-permute-done((f32[14,8,128]{2,1,0:T(8,128)S(1)}, f32[14,8,128]{2,1,0:T(8,128)S(1)}, u32[]{:S(2)}, u32[]{:S(2)}) %collective-permute-start.7) | collective-permute-done | bytes 57376 | tf_op jit(solution)/shard_map/ppermute | solution.py:487
  91.2 11.4 %yee.1 = (f32[3,64,8,128]{3,2,1,0:T(8,128)}, f32[3,64,8,128]{3,2,1,0:T(8,128)}) custom-call(f32[3,64,8,128]{3,2,1,0:T(8,128)S(1)} %copy-done, f32[3,64,8,128]{3,2,1,0:T(8,128)S(1)} %copy-done.1, s32[64,8,128]{2,1,0:T(8,128)S(1)} %copy-done.2, f32[224,8,128]{2,1,0:T(8,128)S(1)} %collective-permute-done.3.up_ref, ...), custom_call_target="tpu_custom_call" | custom-call | flops 40000000 | bytes 8000000 | tf_op jit(solution)/shard_map/yee/pallas_call | solution.py:581
  102.5 1.2 %total.1 = f32[2,512]{1,0:T(2,128)} custom-call(f32[512,128]{1,0:T(8,128)S(1)} %bitcast.6, f32[512,256]{1,0:T(8,128)S(1)} %copy-done.3), custom_call_target="tpu_custom_call" | custom-call | tf_op jit(solution)/shard_map/total/pallas_call | solution.py:619
  (29 shorter events, 0.1 us)
Async XLA Ops:
  0.6 18.6 %copy-start.4 = (f32[128,128]{1,0:T(8,128)S(1)}, f32[128,128]{1,0:T(8,128)}, u32[]{:S(2)}) copy-start(f32[128,128]{1,0:T(8,128)} %constant.23.clone.code_ref) | copy-start | bytes 196612
  0.6 18.6 %copy-start.7 = (f32[8]{0:T(128)S(1)}, f32[8]{0:T(128)}, u32[]{:S(2)}) copy-start(f32[8]{0:T(128)} %eps_ref.3) | copy-start | bytes 100
  0.7 18.6 %copy-start.8 = (f32[8]{0:T(128)S(1)}, f32[8]{0:T(128)}, u32[]{:S(2)}) copy-start(f32[8]{0:T(128)} %sig_ref.3) | copy-start | bytes 100
  0.7 29.8 %copy-start.1 = (f32[3,64,8,128]{3,2,1,0:T(8,128)S(1)}, f32[3,64,8,128]{3,2,1,0:T(8,128)}, u32[]{:S(2)}) copy-start(f32[3,64,8,128]{3,2,1,0:T(8,128)} %h_ref.7) | copy-start | bytes 2359300
  1.8 28.7 %copy-start = (f32[3,64,8,128]{3,2,1,0:T(8,128)S(1)}, f32[3,64,8,128]{3,2,1,0:T(8,128)}, u32[]{:S(2)}) copy-start(f32[3,64,8,128]{3,2,1,0:T(8,128)} %e_ref.7) | copy-start | bytes 2359300
  1.8 17.4 %collective-permute-start = (f32[36,8,128]{2,1,0:T(8,128)S(1)}, f32[36,8,128]{2,1,0:T(8,128)S(1)}, u32[]{:S(2)}, u32[]{:S(2)}) collective-permute-start(f32[36,8,128]{2,1,0:T(8,128)S(1)} %get-tuple-element.16.own_ref), channel_id=1, source_target_pairs={{0,248},{8,0},{16,8},{24,16},{32,24},{40,32},{48,40},{56,48},{64,5... | collective-permute-start | bytes 442376 | tf_op jit(solution)/shard_map/ppermute | solution.py:487
  8.4 9.2 %collective-permute-start.2 = (f32[4,8,128]{2,1,0:T(8,128)S(1)}, f32[4,8,128]{2,1,0:T(8,128)S(1)}, u32[]{:S(2)}, u32[]{:S(2)}) collective-permute-start(f32[4,8,128]{2,1,0:T(8,128)S(1)} %get-tuple-element.17.after_ref), channel_id=1, source_target_pairs={{0,255},{1,248},{2,249},{3,250},{4,251},{5,252},{6,253},{7,254},{8... | collective-permute-start | bytes 49160 | tf_op jit(solution)/shard_map/ppermute | solution.py:497
  9.4 9.9 %collective-permute-start.1 = (f32[4,8,128]{2,1,0:T(8,128)S(1)}, f32[4,8,128]{2,1,0:T(8,128)S(1)}, u32[]{:S(2)}, u32[]{:S(2)}) collective-permute-start(f32[4,8,128]{2,1,0:T(8,128)S(1)} %get-tuple-element.17.after_ref), channel_id=1, source_target_pairs={{0,7},{1,0},{2,1},{3,2},{4,3},{5,4},{6,5},{7,6},{8,15},{9,8},{10,9... | collective-permute-start | bytes 49160 | tf_op jit(solution)/shard_map/ppermute | solution.py:487
  21.6 8.9 %copy-start.2 = (s32[64,8,128]{2,1,0:T(8,128)S(1)}, s32[64,8,128]{2,1,0:T(8,128)}, u32[]{:S(2)}) copy-start(s32[64,8,128]{2,1,0:T(8,128)} %mat_ref.7) | copy-start | bytes 786436
  21.6 28.2 %all-to-all-start = ((bf16[256,8,128]{2,1,0:T(8,128)(2,1)}), bf16[256,8,128]{2,1,0:T(8,128)(2,1)S(1)}, u32[]{:S(2)}, u32[]{:S(2)}) async-start(bf16[256,8,128]{2,1,0:T(8,128)(2,1)} %bitcast.1), calls=%async_computation | async-start | bytes 1048576 | tf_op jit(solution)/shard_map/all_to_all | solution.py:547
  31.4 1.4 %copy-start.5 = (f32[14,8,128]{2,1,0:T(8,128)}, f32[14,8,128]{2,1,0:T(8,128)S(1)}, u32[]{:S(2)}) copy-start(f32[14,8,128]{2,1,0:T(8,128)S(1)} %get-tuple-element.20.after_ref) | copy-start | bytes 172036
  31.4 1.4 %copy-start.9 = (f32[14,8,128]{2,1,0:T(8,128)}, f32[14,8,128]{2,1,0:T(8,128)S(1)}, u32[]{:S(2)}) copy-start(f32[14,8,128]{2,1,0:T(8,128)S(1)} %get-tuple-element.23) | copy-start | bytes 172036
  32.8 58.3 %collective-permute-start.3 = (f32[224,8,128]{2,1,0:T(8,128)}, f32[224,8,128]{2,1,0:T(8,128)S(1)}, u32[]{:S(2)}, u32[]{:S(2)}) collective-permute-start(f32[224,8,128]{2,1,0:T(8,128)} %get-tuple-element.21), channel_id=1, source_target_pairs={{0,8},{8,16},{16,24},{24,32},{32,40},{40,48},{48,56},{56,64},{64,7... | collective-permute-start | bytes 2752520 | tf_op jit(solution)/shard_map/ppermute | solution.py:487
  34.9 56.3 %collective-permute-start.4 = (f32[224,8,128]{2,1,0:T(8,128)}, f32[224,8,128]{2,1,0:T(8,128)}, u32[]{:S(2)}, u32[]{:S(2)}) collective-permute-start(f32[224,8,128]{2,1,0:T(8,128)} %get-tuple-element.22), channel_id=1, source_target_pairs={{8,0},{16,8},{24,16},{32,24},{40,32},{48,40},{56,48},{64,56},{72,6... | collective-permute-start | bytes 2752520 | tf_op jit(solution)/shard_map/ppermute | solution.py:487
  58.5 8.1 %copy-start.10 = (f32[14,8,128]{2,1,0:T(8,128)S(1)}, f32[14,8,128]{2,1,0:T(8,128)}, u32[]{:S(2)}) copy-start(f32[14,8,128]{2,1,0:T(8,128)} %copy-done.9) | copy-start | bytes 172036
  58.5 14.6 %copy-start.6 = (f32[14,8,128]{2,1,0:T(8,128)S(1)}, f32[14,8,128]{2,1,0:T(8,128)}, u32[]{:S(2)}) copy-start(f32[14,8,128]{2,1,0:T(8,128)} %copy-done.5) | copy-start | bytes 172036
  58.5 44.1 %all-to-all-start.1 = ((f32[256,2,128]{2,1,0:T(2,128)}), f32[256,2,128]{2,1,0:T(2,128)S(1)}, u32[]{:S(2)}, u32[]{:S(2)}) async-start(f32[256,2,128]{2,1,0:T(2,128)} %bitcast.3), calls=%async_computation.1 | async-start | bytes 524288 | tf_op jit(solution)/shard_map/all_to_all | solution.py:618
  66.6 8.9 %collective-permute-start.5 = (f32[14,8,128]{2,1,0:T(8,128)S(1)}, f32[14,8,128]{2,1,0:T(8,128)S(1)}, u32[]{:S(2)}, u32[]{:S(2)}) collective-permute-start(f32[14,8,128]{2,1,0:T(8,128)S(1)} %copy-done.10), channel_id=1, source_target_pairs={{0,1},{1,2},{2,3},{3,4},{4,5},{5,6},{6,7},{7,0},{8,9},{9,10},{10,1... | collective-permute-start | bytes 172040 | tf_op jit(solution)/shard_map/ppermute | solution.py:487
  73.0 10.4 %collective-permute-start.6 = (f32[14,8,128]{2,1,0:T(8,128)S(1)}, f32[14,8,128]{2,1,0:T(8,128)S(1)}, u32[]{:S(2)}, u32[]{:S(2)}) collective-permute-start(f32[14,8,128]{2,1,0:T(8,128)S(1)} %copy-done.6), channel_id=1, source_target_pairs={{0,7},{1,0},{2,1},{3,2},{4,3},{5,4},{6,5},{7,6},{8,15},{9,8},{10,9... | collective-permute-start | bytes 172040 | tf_op jit(solution)/shard_map/ppermute | solution.py:487
  83.5 7.6 %collective-permute-start.7 = (f32[14,8,128]{2,1,0:T(8,128)S(1)}, f32[14,8,128]{2,1,0:T(8,128)S(1)}, u32[]{:S(2)}, u32[]{:S(2)}) collective-permute-start(f32[14,8,128]{2,1,0:T(8,128)S(1)} %get-tuple-element.25), channel_id=1, source_target_pairs={{0,8},{8,16},{16,24},{24,32},{32,40},{40,48},{48,56},{56,64},{64,7... | collective-permute-start | bytes 172040 | tf_op jit(solution)/shard_map/ppermute | solution.py:487
  83.6 7.5 %collective-permute-start.8 = (f32[14,8,128]{2,1,0:T(8,128)S(1)}, f32[14,8,128]{2,1,0:T(8,128)S(1)}, u32[]{:S(2)}, u32[]{:S(2)}) collective-permute-start(f32[14,8,128]{2,1,0:T(8,128)S(1)} %get-tuple-element.26), channel_id=1, source_target_pairs={{0,248},{8,0},{16,8},{24,16},{32,24},{40,32},{48,40},{56,48},{64,5... | collective-permute-start | bytes 172040 | tf_op jit(solution)/shard_map/ppermute | solution.py:487
  91.1 11.4 %copy-start.3 = (f32[512,256]{1,0:T(8,128)S(1)}, f32[512,256]{1,0:T(8,128)}, u32[]{:S(2)}) copy-start(f32[512,256]{1,0:T(8,128)} %constant.22.clone.up_ref) | copy-start | bytes 1572868
